TPU v7x, 256 devices: a 4x2x16 block of a 4x16x16 slice. The times are simulated.
256 devices in a mesh: group: 2 (over y), temp: 4 (over x), gz: 32 (over z, core).
Axes of the slice: x: 4, y: 2, z: 16, core: 2. Of those that a mesh axis runs over, the one named last changes fastest.
The devices are a block of a 4x16x16 slice.
Arguments:
- spin_state: float32 [16, 3, 128, 128, 128], P(('group', 'temp'), None, 'gz'), parts along dimension 0, may hold values from -1 to 1, as said below
- couplings: float32 [3, 256, 128, 128], P(None, ('group', 'gz')), parts along dimension 1, may hold values from -12 to 12
- inverse_temps: float32 [16], P(('group', 'temp')), parts along dimension 0, may hold values from 0.3 to 3
- colour_order: int32 [16], P(('group', 'temp')), parts along dimension 0, may hold values 0 or 1
- heat_level: float32 [16, 128, 128, 128], P(('group', 'temp'), 'gz'), parts along dimension 0, may hold values from 0.001 to 0.999
- heat_height: float32 [16, 128, 128, 128], P(('group', 'temp'), 'gz'), parts along dimension 0, may hold values from -1 to 1
- heat_angle: float32 [16, 128, 128, 128], P(('group', 'temp'), 'gz'), parts along dimension 0, may hold values from -3.140625 to 3.140625
- swap_bits: int32 [16], P(('group', 'temp')), parts along dimension 0, may hold values 0 or 1
Outputs:
- spin_final: float32 [16, 3, 128, 128, 128], P(('group', 'temp'), None, 'gz'), parts along dimension 0
- energies: float32 [16], P(('group', 'temp')), parts along dimension 0
There are 2 independent parts, one for each index of `group`. A program takes and returns all parts, laid end to end along the dimension named above; each array names one. Nothing has to cross between parts.
Inputs may be any that keep to these rules, and one draw needn't show every extreme that they name: `spin_state`: every site's three components form a vector of unit length.
All inputs are finite; a program needn't handle non-finite values. No bound on the sum of `colour_order` or of `swap_bits` on one device may be relied on, other than what follows from the above.
Results may differ from a plain program's by a relative error of at most 0.0003.
Values sent between devices are 32-bit elements; how exact they have to be, the bound alone decides.
No kernel may reach another device: no remote copies, remote signals or barrier semaphores. Data moves between devices by JAX's collectives and lax.ppermute only.
A program may use at most 64 MiB of HBM per device.

v0:
```python
import functools

import jax
import jax.numpy as jnp
from jax import lax
from jax.experimental import pallas as pl
from jax.experimental.pallas import tpu as pltpu
from jax.sharding import PartitionSpec as P


F32 = jnp.float32
OR_SWEEPS = 2


VM = pl.BlockSpec(memory_space=pltpu.VMEM)
SM = pl.BlockSpec(memory_space=pltpu.SMEM)
ANY = pl.BlockSpec(memory_space=pl.ANY)
HBM = pl.BlockSpec(memory_space=pltpu.HBM)
PIECES = 9
EARLY = 15
LATE = 9


def vm(*shape, dtype=F32):
    return pltpu.VMEM(shape, dtype)


def kernel_call(body, outs, in_specs, out_specs=None, scratch=(), mib=24):
    return pl.pallas_call(
        body,
        out_shape=outs,
        in_specs=in_specs,
        out_specs=out_specs if out_specs is not None else [VM] * len(outs),
        scratch_shapes=list(scratch),
        compiler_params=pltpu.CompilerParams(vmem_limit_bytes=mib * 1024 * 1024),
    )


def in_hbm(value):
    return pltpu.with_memory_space_constraint(value, pltpu.HBM)


def core_index():
    return lax.rem(lax.axis_index("gz"), 2)


def slot_of(u):
    odd = lax.rem(lax.axis_index("temp"), 2)
    return 1 - odd if u == 0 else odd


def slot_replica(swap, u):
    return slot_of(u) ^ (swap[0] != 0).astype(jnp.int32)


def lane_even(rows, columns, offset):
    lane = lax.broadcasted_iota(jnp.int32, (rows, columns), 1)
    return ((lane + offset) & 1) == 0


def tile(ref, i, half):
    return ref[pl.ds(i * half, half), :]


def put(ref, i, value):
    half = value.shape[0]
    ref[pl.ds(i * half, half), :] = value


def folded(ref, index, half):
    return tuple(ref[(*index, pl.ds(s, half, stride=2), slice(None))] for s in (0, 1))


def folded_rows(ref, base, half):
    return tuple(ref[pl.ds(base + s, half, stride=2), :] for s in (0, 1))


def parity(info, half):
    columns = info.shape[-1]
    lane = lax.broadcasted_iota(jnp.int32, (half, columns), 1)
    return (lane & 1) == jnp.broadcast_to(info[0:1, :], (half, columns))


def at_plane(even, w):
    return even if w % 2 == 0 else jnp.logical_not(even)


def bond_copies(planes, coup, target, base, rows, side_in, sems):
    core = core_index()
    top = planes - 1
    at_top = 1 - core if side_in else core
    z = at_top * top
    return [
        pltpu.make_async_copy(coup.at[d, p], target.at[pl.ds(base + i * rows, rows), :], sems.at[i])
        for i, (d, p) in enumerate(((0, z), (1, z), (2, at_top * (top - 1)), (2, z)))
    ]


def load_kernel(planes, half, *refs):
    (swap_h, colour_h, beta_h, spin_h, coup_h) = refs[:5]
    p0x, p1x, pi, am0, am1, info0, info1, beta0, beta1 = refs[5:14]
    swap, colour, betas, spin, sems, bond_sems = refs[14:]
    core = core_index()
    columns = spin.shape[-1]
    rows = 2 * half
    top = planes - 1
    scalars = [
        pltpu.make_async_copy(swap_h, swap, sems.at[0]),
        pltpu.make_async_copy(colour_h, colour, sems.at[1]),
        pltpu.make_async_copy(beta_h, betas, sems.at[2]),
    ]
    spins = [
        pltpu.make_async_copy(spin_h.at[:, :, w + core * (top - 2 * w)], spin.at[w], sems.at[3 + w])
        for w in range(planes)
    ]
    bonds = bond_copies(planes, coup_h, p0x, PIECES * half, rows, False, bond_sems.at[0])
    bonds += bond_copies(planes, coup_h, pi, 2 * PIECES * half, rows, True, bond_sems.at[1])
    for copy in scalars + spins + bonds:
        copy.start()
    for copy in scalars:
        copy.wait()
    reps, masks = [], []
    for u, info, beta in ((0, info0, beta0), (1, info1, beta1)):
        rep = slot_replica(swap, u)
        c = colour[rep] ^ core
        info[0:1, :] = jnp.full((1, columns), c, jnp.int32)
        info[1:2, :] = jnp.full((1, columns), (swap[1] != 0).astype(jnp.int32), jnp.int32)
        beta[...] = jnp.full(beta.shape, betas[rep], F32)
        reps.append(rep)
        masks.append(lane_even(half, columns, c))
    for w in range(planes):
        spins[w].wait()
        for u, sx, am in ((0, p0x, am0), (1, p1x, am1)):
            base = PIECES * u
            m = at_plane(masks[u], w)
            for k in range(3):
                even, odd = folded(spin, (w, reps[u], k), half)
                a = jnp.where(m, even, odd)
                b = jnp.where(m, odd, even)
                if w == 0:
                    put(sx, k, b)
                    put(sx, 6 + k, a)
                elif w == 1:
                    put(sx, 3 + k, b)
                    put(am, k, a)
                elif w == planes - 2:
                    put(pi, base + 3 + k, b)
                    put(am, 3 + k, a)
                else:
                    put(pi, base + k, b)
                    put(pi, base + 6 + k, a)
    for copy in bonds:
        copy.wait()


def weight_kernel(planes, half, in_chip, *refs):
    coup, sent_ref, info0, info1, weights0, weights1 = refs
    core = core_index()
    top = planes - 1
    rows = 2 * half
    first = core == 0

    def sent(i):
        return folded_rows(sent_ref, (2 if in_chip else 1) * PIECES * half + i * rows, half)

    def zbond(m):
        if m in (-1, planes + 1):
            return sent(2)
        if m in (0, planes):
            ours, theirs = folded(coup, (2, top), half), sent(3)
            mine = first if m == planes else jnp.logical_not(first)
            return tuple(jnp.where(mine, o, t) for o, t in zip(ours, theirs))
        return folded(coup, (2, (m - 1) + core * (top - 2 * m + 1)), half)

    span = range(1, planes + 1) if in_chip else range(-1, 1)
    below = zbond(span[0])
    for i, w in enumerate(span):
        above = zbond(w + 1)
        if w in (-1, planes):
            jx, jy = sent(0), sent(1)
        else:
            z = w + core * (top - 2 * w)
            jx, jy = folded(coup, (0, z), half), folded(coup, (1, z), half)
        up_odd = pltpu.roll(jy[1], 1, 0)
        for info, weights in ((info0, weights0), (info1, weights1)):
            even = parity(info, half)
            for a in (0, 1):
                if a == 1 and w in (-1, planes):
                    continue
                m = at_plane(even, w + a)
                weights[a, i, 0] = jnp.where(m, jx[0], jx[1])
                weights[a, i, 1] = pltpu.roll(jnp.where(m, jx[1], jx[0]), 1, 1)
                weights[a, i, 2] = jy[0]
                weights[a, i, 3] = jnp.where(m, up_odd, jy[1])
                weights[a, i, 4] = jnp.where(m, above[0], above[1])
                weights[a, i, 5] = jnp.where(m, below[0], below[1])
        below = above


def field(get, weight, a, even, w):
    total = []
    m = at_plane(even, w + a)
    for k in range(3):
        o = get(w, k)
        half, columns = o.shape
        side = jnp.where(m, pltpu.roll(o, 1, 0), pltpu.roll(o, half - 1, 0))
        h = weight(a, w, 0) * pltpu.roll(o, columns - 1, 1)
        h = h + weight(a, w, 1) * pltpu.roll(o, 1, 1)
        h = h + weight(a, w, 2) * o
        h = h + weight(a, w, 3) * side
        h = h + weight(a, w, 4) * get(w + 1, k)
        h = h + weight(a, w, 5) * get(w - 1, k)
        total.append(h)
    return total


def weight_of(w_in, w_x):
    return lambda a, w, i: w_in[a, w - 1, i] if w > 0 else w_x[a, w + 1, i]


def dot3(a, b):
    return a[0] * b[0] + a[1] * b[1] + a[2] * b[2]


def reflect(s, h):
    f = 2.0 * dot3(s, h) / jnp.maximum(dot3(h, h), 0.01)
    return [f * h[k] - s[k] for k in range(3)]


def second_planes(planes, half, sx, si, rx, ri, own=0, sent=0):
    def get(w, k):
        if w < 0:
            return tile(rx, 3 * (-1 - w) + k, half)
        if w < 2:
            return tile(sx, 3 * w + k, half)
        if w < planes:
            return tile(si, own + 3 * (planes - 1 - w) + k, half)
        return tile(ri, sent + 3 * (w - planes) + k, half)

    return get


def relax_early(planes, half, first, u, *refs):
    info, w_in, sx, si, ri, a_old = refs[:6]
    a_new, bi = refs[-2:]
    offset = (PIECES if first else 6) * u
    even = parity(info, half)
    weight = weight_of(w_in, None)
    get_b = second_planes(planes, half, sx, si, None, ri, offset, offset)
    if u == 1:
        bi[pl.ds(0, 6 * half), :] = refs[6][...]

    def get_a(w, k):
        if not first:
            return tile(a_old, 3 * (w - 1) + k, half)
        if w == planes - 1:
            return tile(si, offset + 6 + k, half)
        if w == planes:
            return tile(ri, offset + 6 + k, half)
        return tile(a_old, 3 * (w - 1) + k, half)

    for w in range(1, planes + 1):
        h = field(get_b, weight, 0, even, w)
        new = reflect([get_a(w, k) for k in range(3)], h)
        for k in range(3):
            put(a_new, 3 * (w - 1) + k, new[k])
    for w in range(2, planes):
        h = field(lambda v, k: tile(a_new, 3 * (v - 1) + k, half), weight, 1, even, w)
        new = reflect([get_b(w, k) for k in range(3)], h)
        for k in range(3):
            put(bi, 6 * u + 3 * (planes - 1 - w) + k, new[k])


def relax_late(planes, half, first, *refs):
    info, w_in, w_x, sx, rx, a_in = refs[:6]
    a_old, a_new, bx = (None, *refs[6:]) if first else (refs[6], refs[8], refs[7])
    even = parity(info, half)
    weight = weight_of(w_in, w_x)
    get_b = second_planes(planes, half, sx, None, rx, None)

    def get_a(w, k):
        if not first:
            return tile(a_old, 3 * (w + 1) + k, half)
        return tile(rx if w < 0 else sx, 6 + k, half)

    for w in (-1, 0):
        h = field(get_b, weight, 0, even, w)
        new = reflect([get_a(w, k) for k in range(3)], h)
        for k in range(3):
            put(a_new, 3 * (w + 1) + k, new[k])

    def get_new(w, k):
        return tile(a_new, 3 * (w + 1) + k, half) if w < 1 else tile(a_in, 3 * (w - 1) + k, half)

    for w in (0, 1):
        h = field(get_new, weight, 1, even, w)
        new = reflect([get_b(w, k) for k in range(3)], h)
        for k in range(3):
            put(bx, 3 * w + k, new[k])


SIN = (1.0, -1 / 6, 1 / 120, -1 / 5040, 1 / 362880, -1 / 39916800, 1 / 6227020800)
COS = (1.0, -1 / 2, 1 / 24, -1 / 720, 1 / 40320, -1 / 3628800, 1 / 479001600, -1 / 87178291200)


def series(coefficients, y):
    total = coefficients[-1]
    for value in coefficients[-2::-1]:
        total = total * y + value
    return total


def trial(height, angle):
    t = 0.5 * angle
    y = t * t
    s = t * series(SIN, y)
    c = series(COS, y)
    q = jnp.sqrt(jnp.maximum(1.0 - height * height, 0.0))
    return q * (1.0 - 2.0 * (s * s)), q * (2.0 * (s * c))


def trial_kernel(planes, half, swap, colour, level, height, angle, ta0, tb0, ta1, tb1, dx, di):
    core = core_index()
    columns = level.shape[-1]
    for u, ta, tb in ((0, ta0, tb0), (1, ta1, tb1)):
        rep = slot_replica(swap, u)
        c = colour[rep]
        for w in range(planes):
            z = w + core * (planes - 1 - 2 * w)
            m = lane_even(half, columns, z + c)
            a, b = [], []
            for ref in (level, height, angle):
                even, odd = folded(ref, (rep, z), half)
                a.append(jnp.where(m, even, odd))
                b.append(jnp.where(m, odd, even))
            if w == 0 or w == planes - 1:
                for i in range(3):
                    put(dx if w == 0 else di, 3 * u + i, a[i])
            for t, (lev, hei, ang) in ((ta, a), (tb, b)):
                ux, uy = trial(hei, ang)
                t[w, 0], t[w, 1], t[w, 2], t[w, 3] = ux, uy, hei, lev


def trial_of(t, w):
    return [t[w, k] for k in range(3)], t[w, 3]


def trial_sent(draws, u, half):
    level, height, angle = (tile(draws, 3 * u + i, half) for i in range(3))
    ux, uy = trial(height, angle)
    return [ux, uy, height], level


def heated(h, u, level, beta):
    m = jnp.maximum(dot3(h, h), 0.01)
    inverse = lax.rsqrt(m)
    e = [h[k] * inverse for k in range(3)]
    reach = beta * (m * inverse)
    c = 1.0 + jnp.log(1.0 + level * (jnp.exp(-2.0 * reach) - 1.0)) / reach
    along = dot3(u, e)
    t = [u[k] - along * e[k] for k in range(3)]
    f = jnp.sqrt(jnp.maximum(1.0 - c * c, 0.0)) * lax.rsqrt(jnp.maximum(dot3(t, t), 0.0001))
    return [c * e[k] + f * t[k] for k in range(3)]


def heat_early(planes, half, u, *refs):
    info, betas, w_in, sx, si, ri, ta, tb, rdi, out, e_part, halo = refs
    even = parity(info, half)
    columns = info.shape[-1]
    beta = jnp.broadcast_to(betas[0:1, :], (half, columns))
    weight = weight_of(w_in, None)
    get_b = second_planes(planes, half, sx, si, None, ri, 6 * u, 6 * u)

    def get_a(w, k):
        return halo[k] if w == planes else tile(out, 3 * (w - 1) + k, half)

    for w in range(1, planes + 1):
        h = field(get_b, weight, 0, even, w)
        draw = trial_of(ta, w) if w < planes else trial_sent(rdi, u, half)
        new = heated(h, *draw, beta)
        for k in range(3):
            if w == planes:
                halo[k] = new[k]
            else:
                put(out, 3 * (w - 1) + k, new[k])
    energy = None
    for w in range(2, planes):
        h = field(get_a, weight, 1, even, w)
        new = heated(h, *trial_of(tb, w), beta)
        for k in range(3):
            put(out, 9 + 3 * (w - 2) + k, new[k])
        term = dot3(new, h)
        energy = term if energy is None else energy + term
    e_part[...] = energy
    out[pl.ds(EARLY * half, 8), :] = info[...].astype(F32)


def heat_late(planes, half, u, *refs):
    info, betas, w_in, w_x, sx, rx, ta, tb, rdx, inner, e_part = refs[:11]
    if u == 0:
        out, e_out, halo = refs[11:]
    else:
        e_other, out, e_out, halo = refs[11:]
    even = parity(info, half)
    columns = info.shape[-1]
    beta = jnp.broadcast_to(betas[0:1, :], (half, columns))
    weight = weight_of(w_in, w_x)
    get_b = second_planes(planes, half, sx, None, rx, None)

    def get_a(w, k):
        if w < 0:
            return halo[k]
        return tile(out, k, half) if w == 0 else tile(inner, 3 * (w - 1) + k, half)

    for w in (-1, 0):
        h = field(get_b, weight, 0, even, w)
        draw = trial_of(ta, w) if w >= 0 else trial_sent(rdx, u, half)
        new = heated(h, *draw, beta)
        for k in range(3):
            if w < 0:
                halo[k] = new[k]
            else:
                put(out, k, new[k])
    energy = e_part[...]
    for w in (0, 1):
        h = field(get_a, weight, 1, even, w)
        new = heated(h, *trial_of(tb, w), beta)
        for k in range(3):
            put(out, 3 + 3 * w + k, new[k])
        energy = energy + dot3(new, h)
    mine = jnp.full(e_out.shape, -jnp.sum(energy), F32)
    if u == 1:
        lane = lax.broadcasted_iota(jnp.int32, e_out.shape, 1)
        other = jnp.broadcast_to(e_other[0:1, : e_out.shape[1]], e_out.shape)
        mine = jnp.where(lane == 0, other, mine)
    e_out[...] = mine


def exchanged(u, info, note):
    place = lax.axis_index("temp")
    upper = slot_of(u) == 1
    ours = jnp.max(info[1:2, :]) > 0
    theirs = jnp.max(note[1:2, :]) > 0.5
    inside = jnp.where(upper, place != lax.axis_size("temp") - 1, place != 0)
    return jnp.logical_and(jnp.where(upper, ours, theirs), inside)


def out_kernel(planes, half, *refs):
    info0, info1, i0, i1, o0, o1, ri0, ri1, ro0, ro1, out_h, taken, out, sems = refs
    core = core_index()
    columns = out.shape[-1]
    pushes = []
    for u, info, own, other in ((0, info0, (i0, o0), (ri0, ro0)), (1, info1, (i1, o1), (ri1, ro1))):
        note = ri0[pl.ds(EARLY * half, 8), :] if u == 0 else ri1[pl.ds(EARLY * half, 8), :]
        take = exchanged(u, info, note)
        taken[u : u + 1, :] = jnp.full((1, columns), take.astype(jnp.int32), jnp.int32)

        def write(early, late, parities):
            even = (lax.broadcasted_iota(jnp.int32, (half, columns), 1) & 1) == jnp.broadcast_to(
                parities, (half, columns)
            )
            for w in range(planes):
                z = w + core * (planes - 1 - 2 * w)
                m = at_plane(even, w)
                for k in range(3):
                    a = tile(late, k, half) if w == 0 else tile(early, 3 * (w - 1) + k, half)
                    b = tile(late, 3 + 3 * w + k, half) if w < 2 else tile(early, 3 + 3 * w + k, half)
                    out[u, k, z, pl.ds(0, half, stride=2), :] = jnp.where(m, a, b)
                    out[u, k, z, pl.ds(1, half, stride=2), :] = jnp.where(m, b, a)

        @pl.when(take)
        def _():
            write(*other, note[0:1, :].astype(jnp.int32))

        @pl.when(jnp.logical_not(take))
        def _():
            write(*own, info[0:1, :])

        push = pltpu.make_async_copy(out.at[u], out_h.at[slot_of(u)], sems.at[u])
        push.start()
        pushes.append(push)
    for push in pushes:
        push.wait()


def partner_of(u):
    place, temps = lax.axis_index("temp"), lax.axis_size("temp")
    odd = lax.rem(place, 2)
    step = 1 - 2 * odd if u == 0 else 2 * odd - 1
    return lax.rem(place + step + temps, temps)


def energy_kernel(count, sites, taken, parts, energies_h, energies, sem):
    def total(place):
        rows = parts[pl.ds(pl.multiple_of(place * count, count), count), :]
        return jnp.sum(rows, axis=0, keepdims=True) / sites

    own = total(lax.axis_index("temp"))
    final = [
        jnp.where(taken[u : u + 1, u : u + 1] > 0, total(partner_of(u))[:, u : u + 1], own[:, u : u + 1])
        for u in range(2)
    ]
    lane = lax.broadcasted_iota(jnp.int32, energies.shape, 1)
    energies[...] = jnp.where(
        lane == slot_of(0),
        jnp.broadcast_to(final[0], energies.shape),
        jnp.broadcast_to(final[1], energies.shape),
    )
    copy = pltpu.make_async_copy(energies, energies_h, sem)
    copy.start()
    copy.wait()


def step(
    spin_state, couplings, inverse_temps, colour_order, heat_level, heat_height, heat_angle, swap_bits
):
    replicas, _, planes, rows, columns = spin_state.shape
    half = rows // 2
    count = lax.axis_size("gz")
    temps = lax.axis_size("temp")
    assert replicas == 2 and planes == 4 and rows % 2 == 0 and columns % 2 == 0
    assert count % 2 == 0 and temps % 2 == 0
    in_chip = [(i, i ^ 1) for i in range(count)]
    cross = [(i, (i + (1 if i % 2 else -1)) % count) for i in range(count)]
    partners = (
        [(i, i ^ 1) for i in range(temps)],
        [(i, (i + (1 if i % 2 else -1)) % temps) for i in range(temps)],
    )

    def swap_in(value):
        return lax.ppermute(value, "gz", in_chip)

    def swap_cross(value):
        return lax.ppermute(value, "gz", cross)

    def away(value, u):
        return lax.ppermute(value, "temp", partners[u])

    spins = PIECES * half
    pair = vm(6 * half, columns)
    p0x, p1x, pi, am0, am1, info0, info1, beta0, beta1 = kernel_call(
        functools.partial(load_kernel, planes, half),
        [vm(spins + 4 * rows, columns), vm(spins, columns), vm(2 * spins + 4 * rows, columns)]
        + [pair] * 2
        + [vm(8, columns, dtype=jnp.int32)] * 2
        + [vm(8, columns)] * 2,
        [HBM] * 5,
        scratch=[
            pltpu.SMEM((replicas,), jnp.int32),
            pltpu.SMEM((replicas,), jnp.int32),
            pltpu.SMEM((replicas,), F32),
            vm(planes, replicas, 3, rows, columns),
            pltpu.SemaphoreType.DMA((3 + planes,)),
            pltpu.SemaphoreType.DMA((2, 4)),
        ],
    )(*(in_hbm(v) for v in (swap_bits, colour_order, inverse_temps, spin_state, couplings)))
    info, beta = [info0, info1], [beta0, beta1]
    sx, si, a_in, a_x = [p0x, p1x], [pi, pi], [am0, am1], [[], []]
    rx = [swap_cross(sx[u]) for u in range(2)]
    ri = swap_in(pi)

    ta0, tb0, ta1, tb1, dx, di = kernel_call(
        functools.partial(trial_kernel, planes, half),
        [vm(planes, 4, half, columns)] * 4 + [pair] * 2,
        [SM, SM, VM, VM, VM],
    )(swap_bits, colour_order, heat_level, heat_height, heat_angle)
    trial_a, trial_b = [ta0, ta1], [tb0, tb1]
    rdx, rdi = swap_cross(dx), swap_in(di)

    w_in = kernel_call(
        functools.partial(weight_kernel, planes, half, True),
        [vm(2, planes, 6, half, columns)] * 2,
        [VM] * 4,
    )(couplings, ri, info0, info1)
    w_x = kernel_call(
        functools.partial(weight_kernel, planes, half, False),
        [vm(2, 2, 6, half, columns)] * 2,
        [VM] * 4,
    )(couplings, rx[0], info0, info1)

    assert OR_SWEEPS == 2
    for sweep in range(OR_SWEEPS):
        first = sweep == 0
        new_in, bi = [None] * 2, [None] * 2
        for u in range(2):
            new_in[u], bi[u] = kernel_call(
                functools.partial(relax_early, planes, half, first, u),
                [vm(3 * planes * half, columns), vm(6 * (1 + u) * half, columns)],
                [VM] * (6 + u),
            )(info[u], w_in[u], sx[u], si[u], ri, a_in[u], *bi[:u])
        for u in range(2):
            *a_x[u], sx[u] = kernel_call(
                functools.partial(relax_late, planes, half, first),
                [pair] * (1 + first),
                [VM] * (6 if first else 7),
                scratch=[] if first else [pair],
            )(info[u], w_in[u], w_x[u], sx[u], rx[u], new_in[u], *a_x[u])
            si[u], a_in[u] = bi[u], new_in[u]
            rx[u] = swap_cross(sx[u])
        ri = swap_in(bi[1])

    inner, outer, part, r_inner, r_outer = ([None] * 2 for _ in range(5))
    for u in range(2):
        inner[u], part[u] = kernel_call(
            functools.partial(heat_early, planes, half, u),
            [vm(EARLY * half + 8, columns), vm(half, columns)],
            [VM] * 9,
            scratch=[vm(3, half, columns)],
        )(info[u], beta[u], w_in[u], sx[u], si[u], ri, trial_a[u], trial_b[u], rdi)
        r_inner[u] = away(inner[u], u)
    energy = []
    for u in range(2):
        outer[u], *energy = kernel_call(
            functools.partial(heat_late, planes, half, u),
            [vm(LATE * half, columns), vm(temps * count, 2) if u else vm(8, columns)],
            [VM] * (11 + u),
            scratch=[vm(3, half, columns)],
        )(
            info[u], beta[u], w_in[u], w_x[u], sx[u], rx[u],
            trial_a[u], trial_b[u], rdx, inner[u], part[u], *energy,
        )
        r_outer[u] = away(outer[u], u)

    parts = lax.all_to_all(energy[0], ("temp", "gz"), split_axis=0, concat_axis=0, tiled=True)

    spin_final, taken = kernel_call(
        functools.partial(out_kernel, planes, half),
        [jax.ShapeDtypeStruct(spin_state.shape, F32), vm(8, columns, dtype=jnp.int32)],
        [VM] * 10,
        out_specs=[HBM, VM],
        scratch=[vm(*spin_state.shape), pltpu.SemaphoreType.DMA((2,))],
    )(info0, info1, *inner, *outer, *r_inner, *r_outer)
    (energies,) = kernel_call(
        functools.partial(energy_kernel, count, float(columns * rows * planes * count)),
        [jax.ShapeDtypeStruct((1, 2), F32)],
        [VM] * 2,
        out_specs=[HBM],
        scratch=[vm(1, 2), pltpu.SemaphoreType.DMA(())],
    )(taken, parts)
    return spin_final, energies.reshape(-1)


def solution(mesh):
    return jax.shard_map(
        step,
        mesh=mesh,
        in_specs=(
            P(("group", "temp"), None, "gz", None, None),
            P(None, ("group", "gz"), None, None),
            P(("group", "temp")),
            P(("group", "temp")),
            P(("group", "temp"), "gz", None, None),
            P(("group", "temp"), "gz", None, None),
            P(("group", "temp"), "gz", None, None),
            P(("group", "temp")),
        ),
        out_specs=(P(("group", "temp"), None, "gz", None, None), P(("group", "temp"))),
        check_vma=False,
    )
```

profile of v0, /device:TPU:40, one launch (start us, length us, event | category | flops | bytes accessed | tf_op | source)
XLA Modules:
  0.0 91.1 jit_solution(2745119705167135231)
XLA Ops:
  0.6 1.8 %shard_map.95 = (f32[1088,128]{1,0:T(8,128)S(1)}, f32[576,128]{1,0:T(8,128)S(1)}, f32[1664,128]{1,0:T(8,128)S(1)}, f32[384,128]{1,0:T(8,128)S(1)}, f32[384,128]{...) custom-call(s32[2]{0:T(128)} %swap.1, s32[2]{0:T(128)} %colour.1, ...), custom_call_target="tpu_custom_call" | custom-call | tf_op jit(solution)/shard_map/pallas_call | solution.py:541
  2.6 22.5 %collective-permute-start.1 = (f32[1088,128]{1,0:T(8,128)S(1)}, f32[1088,128]{1,0:T(8,128)S(1)}, u32[]{:S(2)}, u32[]{:S(2)}) collective-permute-start(f32[1088,128]{1,0:T(8,128)S(1)} %get-tuple-element.48.refs_2_.refs_3_), channel_id=1, source_target_pairs={{0,31},{1,2},{2,1},{3,4},{4,3},{5,6},{6,5},{7,8},{8,7},{9,10},{10,... | collective-permute-start | bytes 1671176 | tf_op jit(solution)/shard_map/ppermute | solution.py:534
  26.7 2.3 %collective-permute-start.4 = (f32[576,128]{1,0:T(8,128)S(1)}, f32[576,128]{1,0:T(8,128)S(1)}, u32[]{:S(2)}, u32[]{:S(2)}) collective-permute-start(f32[576,128]{1,0:T(8,128)S(1)} %get-tuple-element.55.refs_2_.refs_3_), channel_id=1, source_target_pairs={{0,31},{1,2},{2,1},{3,4},{4,3},{5,6},{6,5},{7,8},{8,7},{9,10},{10,... | collective-permute-start | bytes 884744 | tf_op jit(solution)/shard_map/ppermute | solution.py:534
  29.1 3.2 %collective-permute-done.1.refs_1_.refs_4_ = f32[1088,128]{1,0:T(8,128)S(1)} collective-permute-done((f32[1088,128]{1,0:T(8,128)S(1)}, f32[1088,128]{1,0:T(8,128)S(1)}, u32[]{:S(2)}, u32[]{:S(2)}) %collective-permute-start.1) | collective-permute-done | bytes 557088 | tf_op jit(solution)/shard_map/ppermute | solution.py:534
  32.9 2.5 %collective-permute-done.4.refs_4_ = f32[576,128]{1,0:T(8,128)S(1)} collective-permute-done((f32[576,128]{1,0:T(8,128)S(1)}, f32[576,128]{1,0:T(8,128)S(1)}, u32[]{:S(2)}, u32[]{:S(2)}) %collective-permute-start.4) | collective-permute-done | bytes 294944 | tf_op jit(solution)/shard_map/ppermute | solution.py:534
  37.4 3.1 %collective-permute-start.2 = (f32[384,128]{1,0:T(8,128)S(1)}, f32[384,128]{1,0:T(8,128)S(1)}, u32[]{:S(2)}, u32[]{:S(2)}) collective-permute-start(f32[384,128]{1,0:T(8,128)S(1)} %get-tuple-element.52.refs_2_.refs_3_), channel_id=1, source_target_pairs={{0,31},{1,2},{2,1},{3,4},{4,3},{5,6},{6,5},{7,8},{8,7},{9,10},{10,... | collective-permute-start | bytes 589832 | tf_op jit(solution)/shard_map/ppermute | solution.py:534
  40.7 1.4 %shard_map.105 = (f32[4,4,64,128]{3,2,1,0:T(8,128)S(1)}, f32[4,4,64,128]{3,2,1,0:T(8,128)S(1)}, f32[4,4,64,128]{3,2,1,0:T(8,128)S(1)}, f32[4,4,64,128]{3,2,1,0:T...) custom-call(s32[2]{0:T(128)S(1)} %copy-done.4, s32[2]{0:T(128)S(1)} %copy-done.5, ...), custom_call_target="tpu_custom_call" | custom-call | tf_op jit(solution)/shard_map/pallas_call | solution.py:562
  42.2 1.6 %collective-permute-done.2.refs_4_ = f32[384,128]{1,0:T(8,128)S(1)} collective-permute-done((f32[384,128]{1,0:T(8,128)S(1)}, f32[384,128]{1,0:T(8,128)S(1)}, u32[]{:S(2)}, u32[]{:S(2)}) %collective-permute-start.2) | collective-permute-done | bytes 196640 | tf_op jit(solution)/shard_map/ppermute | solution.py:534
  44.3 2.5 %collective-permute-done.7.refs_4_ = f32[384,128]{1,0:T(8,128)S(1)} collective-permute-done((f32[384,128]{1,0:T(8,128)S(1)}, f32[384,128]{1,0:T(8,128)S(1)}, u32[]{:S(2)}, u32[]{:S(2)}) %collective-permute-start.7) | collective-permute-done | bytes 196640 | tf_op jit(solution)/shard_map/ppermute | solution.py:534
  47.3 0.9 %shard_map.106 = (f32[968,128]{1,0:T(8,128)S(1)}, f32[64,128]{1,0:T(8,128)S(1)}) custom-call(s32[8,128]{1,0:T(8,128)S(1)} %get-tuple-element.43.refs_2_.refs_0_, f32[8,128]{1,0:T(8,128)S(1)} %get-tuple-element.45.refs_1_, f32[2,4,6,64,128]{4,3,2,1,0:T(8,128)S(1)} %get-tuple-element.47.refs_1_.refs_2_, f32[384,128]{1,0:T(8,128)S(1)} %shard_map.102.refs_3_.refs_4_, ...), custom_call_target="tpu_custom_call" | custom-call | tf_op jit(solution)/shard_map/pallas_call | solution.py:604
  48.2 1.9 %collective-permute-start.11 = (f32[968,128]{1,0:T(8,128)S(1)}, f32[968,128]{1,0:T(8,128)S(1)}, u32[]{:S(2)}, u32[]{:S(2)}) collective-permute-start(f32[968,128]{1,0:T(8,128)S(1)} %get-tuple-element.68.refs_9_.refs_2_), channel_id=1, source_target_pairs={{0,32},{32,0},{64,96},{96,64},{1,33},{33,1},{65,97},{97,65},{2,34}... | collective-permute-start | bytes 1486856 | tf_op jit(solution)/shard_map/ppermute | solution.py:537
  50.2 1.0 %shard_map.108 = (f32[968,128]{1,0:T(8,128)S(1)}, f32[64,128]{1,0:T(8,128)S(1)}) custom-call(s32[8,128]{1,0:T(8,128)S(1)} %get-tuple-element.44.refs_3_.refs_0_.refs_1_, f32[8,128]{1,0:T(8,128)S(1)} %get-tuple-element.69.refs_1_, f32[2,4,6,64,128]{4,3,2,1,0:T(8,128)S(1)} %get-tuple-element.54.refs_1_.refs_2_, f32[384,128]{1,0:T(8,128)S(1)} %shard_map.107.refs_3_.refs_4_, ...), custom_call_target="tpu_custom_call" | custom-call | tf_op jit(solution)/shard_map/pallas_call | solution.py:604
  51.1 2.4 %collective-permute-start.12 = (f32[968,128]{1,0:T(8,128)S(1)}, f32[968,128]{1,0:T(8,128)S(1)}, u32[]{:S(2)}, u32[]{:S(2)}) collective-permute-start(f32[968,128]{1,0:T(8,128)S(1)} %get-tuple-element.74.refs_9_.refs_3_), channel_id=1, source_target_pairs={{0,96},{32,64},{64,32},{96,0},{1,97},{33,65},{65,33},{97,1},{2,98}... | collective-permute-start | bytes 1486856 | tf_op jit(solution)/shard_map/ppermute | solution.py:537
  53.5 1.5 %collective-permute-start.9 = (f32[384,128]{1,0:T(8,128)S(1)}, f32[384,128]{1,0:T(8,128)S(1)}, u32[]{:S(2)}, u32[]{:S(2)}) collective-permute-start(f32[384,128]{1,0:T(8,128)S(1)} %get-tuple-element.75), channel_id=1, source_target_pairs={{0,31},{1,2},{2,1},{3,4},{4,3},{5,6},{6,5},{7,8},{8,7},{9,10},{10,... | collective-permute-start | bytes 589832 | tf_op jit(solution)/shard_map/ppermute | solution.py:534
  55.0 1.4 %collective-permute-start.8 = (f32[384,128]{1,0:T(8,128)S(1)}, f32[384,128]{1,0:T(8,128)S(1)}, u32[]{:S(2)}, u32[]{:S(2)}) collective-permute-start(f32[384,128]{1,0:T(8,128)S(1)} %shard_map.102.refs_3_.refs_4_), channel_id=1, source_target_pairs={{0,31},{1,2},{2,1},{3,4},{4,3},{5,6},{6,5},{7,8},{8,7},{9,10},{10,... | collective-permute-start | bytes 589832 | tf_op jit(solution)/shard_map/ppermute | solution.py:534
  56.5 1.5 %collective-permute-start.10 = (f32[384,128]{1,0:T(8,128)S(1)}, f32[384,128]{1,0:T(8,128)S(1)}, u32[]{:S(2)}, u32[]{:S(2)}) collective-permute-start(f32[384,128]{1,0:T(8,128)S(1)} %shard_map.107.refs_3_.refs_4_), channel_id=1, source_target_pairs={{0,31},{1,2},{2,1},{3,4},{4,3},{5,6},{6,5},{7,8},{8,7},{9,10},{10,... | collective-permute-start | bytes 589832 | tf_op jit(solution)/shard_map/ppermute | solution.py:534
  58.0 1.8 %collective-permute-done.9.refs_8_ = f32[384,128]{1,0:T(8,128)S(1)} collective-permute-done((f32[384,128]{1,0:T(8,128)S(1)}, f32[384,128]{1,0:T(8,128)S(1)}, u32[]{:S(2)}, u32[]{:S(2)}) %collective-permute-start.9) | collective-permute-done | bytes 196640 | tf_op jit(solution)/shard_map/ppermute | solution.py:534
  59.8 2.1 %collective-permute-done.8.refs_5_ = f32[384,128]{1,0:T(8,128)S(1)} collective-permute-done((f32[384,128]{1,0:T(8,128)S(1)}, f32[384,128]{1,0:T(8,128)S(1)}, u32[]{:S(2)}, u32[]{:S(2)}) %collective-permute-start.8) | collective-permute-done | bytes 196640 | tf_op jit(solution)/shard_map/ppermute | solution.py:534
  62.7 0.9 collective-permute-start.13
  64.0 1.4 %shard_map.110 = (f32[576,128]{1,0:T(8,128)S(1)}, f32[128,2]{1,0:T(8,128)}) custom-call(s32[8,128]{1,0:T(8,128)S(1)} %get-tuple-element.44.refs_3_.refs_0_.refs_1_, f32[8,128]{1,0:T(8,128)S(1)} %get-tuple-element.69.refs_1_, f32[2,4,6,64,128]{4,3,2,1,0:T(8,128)S(1)} %get-tuple-element.54.refs_1_.refs_2_, ...), custom_call_target="tpu_custom_call" | custom-call | tf_op jit(solution)/shard_map/pallas_call | solution.py:613
  65.4 1.0 %collective-permute-start.14 = (f32[576,128]{1,0:T(8,128)S(1)}, f32[576,128]{1,0:T(8,128)S(1)}, u32[]{:S(2)}, u32[]{:S(2)}) collective-permute-start(f32[576,128]{1,0:T(8,128)S(1)} %get-tuple-element.80.refs_5_), channel_id=1, source_target_pairs={{0,96},{32,64},{64,32},{96,0},{1,97},{33,65},{65,33},{97,1},{2,98}... | collective-permute-start | bytes 884744 | tf_op jit(solution)/shard_map/ppermute | solution.py:537
  66.4 10.3 %all-to-all-start = ((f32[128,1,2]{2,1,0:T(1,128)}), f32[128,1,2]{2,1,0:T(1,128)S(1)}, u32[]{:S(2)}, u32[]{:S(2)}) async-start(f32[128,1,2]{2,1,0:T(1,128)} %bitcast.1), calls=%async_computation | async-start | bytes 131072 | tf_op jit(solution)/shard_map/all_to_all | solution.py:624
  76.7 1.4 %shard_map.111 = (f32[2,3,4,128,128]{4,3,2,1,0:T(8,128)}, s32[8,128]{1,0:T(8,128)S(1)}) custom-call(s32[8,128]{1,0:T(8,128)S(1)} %get-tuple-element.43.refs_2_.refs_0_, s32[8,128]{1,0:T(8,128)S(1)} %get-tuple-element.44.refs_3_.refs_0_.refs_1_, f32[968,128]{1,0:T(8,128)S(1)} %get-tuple-element.68.refs_9_.refs_2_, ...), custom_call_target="tpu_custom_call" | custom-call | tf_op jit(solution)/shard_map/pallas_call | solution.py:626
  78.2 12.1 %all-to-all-done = f32[128,1,2]{2,1,0:T(1,128)S(1)} async-done(((f32[128,1,2]{2,1,0:T(1,128)}), f32[128,1,2]{2,1,0:T(1,128)S(1)}, u32[]{:S(2)}, u32[]{:S(2)}) %all-to-all-start) | async-done | bytes 1056 | tf_op jit(solution)/shard_map/all_to_all | solution.py:624
  (38 shorter events, 7.4 us)
Async XLA Ops:
  0.6 24.4 %copy-start = (f32[3,4,128,128]{3,2,1,0:T(8,128)S(1)}, f32[3,4,128,128]{3,2,1,0:T(8,128)}, u32[]{:S(2)}) copy-start(f32[3,4,128,128]{3,2,1,0:T(8,128)} %refs_0_.5) | copy-start | bytes 2359300
  2.4 22.6 %collective-permute-start = (f32[1664,128]{1,0:T(8,128)S(1)}, f32[1664,128]{1,0:T(8,128)S(1)}, u32[]{:S(2)}, u32[]{:S(2)}) collective-permute-start(f32[1664,128]{1,0:T(8,128)S(1)} %get-tuple-element.46.refs_3_), channel_id=1, source_target_pairs={{0,1},{1,0},{2,3},{3,2},{4,5},{5,4},{6,7},{7,6},{8,9},{9,8},{10,11... | collective-permute-start | bytes 2555912 | tf_op jit(solution)/shard_map/ppermute | solution.py:531
  2.6 29.7 %collective-permute-start.1 = (f32[1088,128]{1,0:T(8,128)S(1)}, f32[1088,128]{1,0:T(8,128)S(1)}, u32[]{:S(2)}, u32[]{:S(2)}) collective-permute-start(f32[1088,128]{1,0:T(8,128)S(1)} %get-tuple-element.48.refs_2_.refs_3_), channel_id=1, source_target_pairs={{0,31},{1,2},{2,1},{3,4},{4,3},{5,6},{6,5},{7,8},{8,7},{9,10},{10,... | collective-permute-start | bytes 1671176 | tf_op jit(solution)/shard_map/ppermute | solution.py:534
  26.6 9.3 %collective-permute-start.3 = (f32[768,128]{1,0:T(8,128)S(1)}, f32[768,128]{1,0:T(8,128)S(1)}, u32[]{:S(2)}, u32[]{:S(2)}) collective-permute-start(f32[768,128]{1,0:T(8,128)S(1)} %get-tuple-element.57.refs_3_), channel_id=1, source_target_pairs={{0,1},{1,0},{2,3},{3,2},{4,5},{5,4},{6,7},{7,6},{8,9},{9,8},{10,11... | collective-permute-start | bytes 1179656 | tf_op jit(solution)/shard_map/ppermute | solution.py:531
  26.7 8.7 %collective-permute-start.4 = (f32[576,128]{1,0:T(8,128)S(1)}, f32[576,128]{1,0:T(8,128)S(1)}, u32[]{:S(2)}, u32[]{:S(2)}) collective-permute-start(f32[576,128]{1,0:T(8,128)S(1)} %get-tuple-element.55.refs_2_.refs_3_), channel_id=1, source_target_pairs={{0,31},{1,2},{2,1},{3,4},{4,3},{5,6},{6,5},{7,8},{8,7},{9,10},{10,... | collective-permute-start | bytes 884744 | tf_op jit(solution)/shard_map/ppermute | solution.py:534
  36.6 4.1 %copy-start.1 = (f32[2,4,128,128]{3,2,1,0:T(8,128)S(1)}, f32[2,4,128,128]{3,2,1,0:T(8,128)}, u32[]{:S(2)}) copy-start(f32[2,4,128,128]{3,2,1,0:T(8,128)} %level.1) | copy-start | bytes 1572868
  36.6 4.0 %copy-start.2 = (f32[2,4,128,128]{3,2,1,0:T(8,128)S(1)}, f32[2,4,128,128]{3,2,1,0:T(8,128)}, u32[]{:S(2)}) copy-start(f32[2,4,128,128]{3,2,1,0:T(8,128)} %height.1) | copy-start | bytes 1572868
  36.6 4.0 %copy-start.3 = (f32[2,4,128,128]{3,2,1,0:T(8,128)S(1)}, f32[2,4,128,128]{3,2,1,0:T(8,128)}, u32[]{:S(2)}) copy-start(f32[2,4,128,128]{3,2,1,0:T(8,128)} %angle.1) | copy-start | bytes 1572868
  36.6 4.0 %copy-start.4 = (s32[2]{0:T(128)S(1)}, s32[2]{0:T(128)}, u32[]{:S(2)}) copy-start(s32[2]{0:T(128)} %swap.1) | copy-start | bytes 28
  36.6 4.0 %copy-start.5 = (s32[2]{0:T(128)S(1)}, s32[2]{0:T(128)}, u32[]{:S(2)}) copy-start(s32[2]{0:T(128)} %colour.1) | copy-start | bytes 28
  37.3 10.0 %collective-permute-start.5 = (f32[768,128]{1,0:T(8,128)S(1)}, f32[768,128]{1,0:T(8,128)S(1)}, u32[]{:S(2)}, u32[]{:S(2)}) collective-permute-start(f32[768,128]{1,0:T(8,128)S(1)} %get-tuple-element.64.refs_4_), channel_id=1, source_target_pairs={{0,1},{1,0},{2,3},{3,2},{4,5},{5,4},{6,7},{7,6},{8,9},{9,8},{10,11... | collective-permute-start | bytes 1179656 | tf_op jit(solution)/shard_map/ppermute | solution.py:531
  37.4 6.4 %collective-permute-start.2 = (f32[384,128]{1,0:T(8,128)S(1)}, f32[384,128]{1,0:T(8,128)S(1)}, u32[]{:S(2)}, u32[]{:S(2)}) collective-permute-start(f32[384,128]{1,0:T(8,128)S(1)} %get-tuple-element.52.refs_2_.refs_3_), channel_id=1, source_target_pairs={{0,31},{1,2},{2,1},{3,4},{4,3},{5,6},{6,5},{7,8},{8,7},{9,10},{10,... | collective-permute-start | bytes 589832 | tf_op jit(solution)/shard_map/ppermute | solution.py:534
  40.5 6.3 %collective-permute-start.7 = (f32[384,128]{1,0:T(8,128)S(1)}, f32[384,128]{1,0:T(8,128)S(1)}, u32[]{:S(2)}, u32[]{:S(2)}) collective-permute-start(f32[384,128]{1,0:T(8,128)S(1)} %get-tuple-element.63.refs_2_.refs_3_), channel_id=1, source_target_pairs={{0,31},{1,2},{2,1},{3,4},{4,3},{5,6},{6,5},{7,8},{8,7},{9,10},{10,... | collective-permute-start | bytes 589832 | tf_op jit(solution)/shard_map/ppermute | solution.py:534
  42.1 5.2 %collective-permute-start.6 = (f32[384,128]{1,0:T(8,128)S(1)}, f32[384,128]{1,0:T(8,128)S(1)}, u32[]{:S(2)}, u32[]{:S(2)}) collective-permute-start(f32[384,128]{1,0:T(8,128)S(1)} %get-tuple-element.67), channel_id=1, source_target_pairs={{0,1},{1,0},{2,3},{3,2},{4,5},{5,4},{6,7},{7,6},{8,9},{9,8},{10,11... | collective-permute-start | bytes 589832 | tf_op jit(solution)/shard_map/ppermute | solution.py:531
  48.2 28.5 %collective-permute-start.11 = (f32[968,128]{1,0:T(8,128)S(1)}, f32[968,128]{1,0:T(8,128)S(1)}, u32[]{:S(2)}, u32[]{:S(2)}) collective-permute-start(f32[968,128]{1,0:T(8,128)S(1)} %get-tuple-element.68.refs_9_.refs_2_), channel_id=1, source_target_pairs={{0,32},{32,0},{64,96},{96,64},{1,33},{33,1},{65,97},{97,65},{2,34}... | collective-permute-start | bytes 1486856 | tf_op jit(solution)/shard_map/ppermute | solution.py:537
  51.1 25.6 %collective-permute-start.12 = (f32[968,128]{1,0:T(8,128)S(1)}, f32[968,128]{1,0:T(8,128)S(1)}, u32[]{:S(2)}, u32[]{:S(2)}) collective-permute-start(f32[968,128]{1,0:T(8,128)S(1)} %get-tuple-element.74.refs_9_.refs_3_), channel_id=1, source_target_pairs={{0,96},{32,64},{64,32},{96,0},{1,97},{33,65},{65,33},{97,1},{2,98}... | collective-permute-start | bytes 1486856 | tf_op jit(solution)/shard_map/ppermute | solution.py:537
  53.5 6.3 %collective-permute-start.9 = (f32[384,128]{1,0:T(8,128)S(1)}, f32[384,128]{1,0:T(8,128)S(1)}, u32[]{:S(2)}, u32[]{:S(2)}) collective-permute-start(f32[384,128]{1,0:T(8,128)S(1)} %get-tuple-element.75), channel_id=1, source_target_pairs={{0,31},{1,2},{2,1},{3,4},{4,3},{5,6},{6,5},{7,8},{8,7},{9,10},{10,... | collective-permute-start | bytes 589832 | tf_op jit(solution)/shard_map/ppermute | solution.py:534
  55.0 6.9 %collective-permute-start.8 = (f32[384,128]{1,0:T(8,128)S(1)}, f32[384,128]{1,0:T(8,128)S(1)}, u32[]{:S(2)}, u32[]{:S(2)}) collective-permute-start(f32[384,128]{1,0:T(8,128)S(1)} %shard_map.102.refs_3_.refs_4_), channel_id=1, source_target_pairs={{0,31},{1,2},{2,1},{3,4},{4,3},{5,6},{6,5},{7,8},{8,7},{9,10},{10,... | collective-permute-start | bytes 589832 | tf_op jit(solution)/shard_map/ppermute | solution.py:534
  56.5 7.6 %collective-permute-start.10 = (f32[384,128]{1,0:T(8,128)S(1)}, f32[384,128]{1,0:T(8,128)S(1)}, u32[]{:S(2)}, u32[]{:S(2)}) collective-permute-start(f32[384,128]{1,0:T(8,128)S(1)} %shard_map.107.refs_3_.refs_4_), channel_id=1, source_target_pairs={{0,31},{1,2},{2,1},{3,4},{4,3},{5,6},{6,5},{7,8},{8,7},{9,10},{10,... | collective-permute-start | bytes 589832 | tf_op jit(solution)/shard_map/ppermute | solution.py:534
  62.7 14.0 %collective-permute-start.13 = (f32[576,128]{1,0:T(8,128)S(1)}, f32[576,128]{1,0:T(8,128)S(1)}, u32[]{:S(2)}, u32[]{:S(2)}) collective-permute-start(f32[576,128]{1,0:T(8,128)S(1)} %get-tuple-element.77.refs_4_), channel_id=1, source_target_pairs={{0,32},{32,0},{64,96},{96,64},{1,33},{33,1},{65,97},{97,65},{2,34}... | collective-permute-start | bytes 884744 | tf_op jit(solution)/shard_map/ppermute | solution.py:537
  65.4 11.3 %collective-permute-start.14 = (f32[576,128]{1,0:T(8,128)S(1)}, f32[576,128]{1,0:T(8,128)S(1)}, u32[]{:S(2)}, u32[]{:S(2)}) collective-permute-start(f32[576,128]{1,0:T(8,128)S(1)} %get-tuple-element.80.refs_5_), channel_id=1, source_target_pairs={{0,96},{32,64},{64,32},{96,0},{1,97},{33,65},{65,33},{97,1},{2,98}... | collective-permute-start | bytes 884744 | tf_op jit(solution)/shard_map/ppermute | solution.py:537
  66.4 23.9 %all-to-all-start = ((f32[128,1,2]{2,1,0:T(1,128)}), f32[128,1,2]{2,1,0:T(1,128)S(1)}, u32[]{:S(2)}, u32[]{:S(2)}) async-start(f32[128,1,2]{2,1,0:T(1,128)} %bitcast.1), calls=%async_computation | async-start | bytes 131072 | tf_op jit(solution)/shard_map/all_to_all | solution.py:624
where the time goes:
time: 91.4 us; the launch traced here: 91.1 us
  starting transfers between devices  49.5 us (54%)
  waiting for transfers between devices  26.4 us (29%)
  Pallas kernels  14.1 us (15%)
  between operations  1.05 us (1%)
    ppermute x7, starting transfers between devices, swap_cross(): return lax.ppermute(value, 'gz', cross)  32.5 us
    ppermute x7, waiting for transfers between devices, swap_cross(): return lax.ppermute(value, 'gz', cross)  14.2 us
    all_to_all x1, waiting for transfers between devices, step(): lax.all_to_all(energy[0], ('temp', 'gz'), split_axis=0, concat_axis=0, ti...  12.1 us
    all_to_all x1, starting transfers between devices, step(): lax.all_to_all(energy[0], ('temp', 'gz'), split_axis=0, concat_axis=0, ti...  10.3 us
    ppermute x4, starting transfers between devices, away(): return lax.ppermute(value, 'temp', partners[u])  6.14 us
    pallas_call x4, Pallas kernels, step(): kernel_call(functools.partial(relax_early, planes, half, first, u), [vm(3...  2.51 us
    pallas_call x2, Pallas kernels, step(): kernel_call(functools.partial(heat_late, planes, half, u), [vm(LATE * hal...  2.14 us
    pallas_call x2, Pallas kernels, step(): kernel_call(functools.partial(heat_early, planes, half, u), [vm(EARLY * h...  1.9 us
  transfers between devices with their start and end apart: 16, of which 8 were waited for; matrix products, arithmetic and copies ran while one was open for 0% of the time, Pallas kernels for 10%

commit v1 on v0

--- a/solution.py
+++ b/solution.py
@@ -96,59 +96,58 @@
     ]
 
 
-def load_kernel(planes, half, *refs):
-    (swap_h, colour_h, beta_h, spin_h, coup_h) = refs[:5]
-    p0x, p1x, pi, am0, am1, info0, info1, beta0, beta1 = refs[5:14]
-    swap, colour, betas, spin, sems, bond_sems = refs[14:]
+def load_kernel(planes, half, in_chip, *refs):
+    swap_h, colour_h, beta_h, spin_h, coup_h = refs[:5]
+    if in_chip:
+        pi, am0, am1 = refs[5:8]
+    else:
+        p0x, p1x, am0, am1, info0, info1, beta0, beta1 = refs[5:13]
+    swap, colour, betas, spin, sems, bond_sems = refs[-6:]
     core = core_index()
     columns = spin.shape[-1]
     rows = 2 * half
     top = planes - 1
+    sides = (planes - 1, planes - 2) if in_chip else (0, 1)
     scalars = [
         pltpu.make_async_copy(swap_h, swap, sems.at[0]),
         pltpu.make_async_copy(colour_h, colour, sems.at[1]),
         pltpu.make_async_copy(beta_h, betas, sems.at[2]),
     ]
     spins = [
-        pltpu.make_async_copy(spin_h.at[:, :, w + core * (top - 2 * w)], spin.at[w], sems.at[3 + w])
-        for w in range(planes)
+        pltpu.make_async_copy(spin_h.at[:, :, w + core * (top - 2 * w)], spin.at[i], sems.at[3 + i])
+        for i, w in enumerate(sides)
     ]
-    bonds = bond_copies(planes, coup_h, p0x, PIECES * half, rows, False, bond_sems.at[0])
-    bonds += bond_copies(planes, coup_h, pi, 2 * PIECES * half, rows, True, bond_sems.at[1])
+    payload, base = (pi, 2 * PIECES * half) if in_chip else (p0x, PIECES * half)
+    bonds = bond_copies(planes, coup_h, payload, base, rows, in_chip, bond_sems)
     for copy in scalars + spins + bonds:
         copy.start()
     for copy in scalars:
         copy.wait()
     reps, masks = [], []
-    for u, info, beta in ((0, info0, beta0), (1, info1, beta1)):
+    for u in range(2):
         rep = slot_replica(swap, u)
         c = colour[rep] ^ core
-        info[0:1, :] = jnp.full((1, columns), c, jnp.int32)
-        info[1:2, :] = jnp.full((1, columns), (swap[1] != 0).astype(jnp.int32), jnp.int32)
-        beta[...] = jnp.full(beta.shape, betas[rep], F32)
+        if not in_chip:
+            info, beta = ((info0, beta0), (info1, beta1))[u]
+            info[0:1, :] = jnp.full((1, columns), c, jnp.int32)
+            info[1:2, :] = jnp.full((1, columns), (swap[1] != 0).astype(jnp.int32), jnp.int32)
+            beta[...] = jnp.full(beta.shape, betas[rep], F32)
         reps.append(rep)
         masks.append(lane_even(half, columns, c))
-    for w in range(planes):
-        spins[w].wait()
-        for u, sx, am in ((0, p0x, am0), (1, p1x, am1)):
-            base = PIECES * u
+    for i, w in enumerate(sides):
+        spins[i].wait()
+        for u, am in ((0, am0), (1, am1)):
+            side, base = (pi, PIECES * u) if in_chip else ((p0x, p1x)[u], 0)
             m = at_plane(masks[u], w)
             for k in range(3):
-                even, odd = folded(spin, (w, reps[u], k), half)
+                even, odd = folded(spin, (i, reps[u], k), half)
                 a = jnp.where(m, even, odd)
                 b = jnp.where(m, odd, even)
-                if w == 0:
-                    put(sx, k, b)
-                    put(sx, 6 + k, a)
-                elif w == 1:
-                    put(sx, 3 + k, b)
+                put(side, base + 3 * i + k, b)
+                if i == 0:
+                    put(side, base + 6 + k, a)
+                else:
                     put(am, k, a)
-                elif w == planes - 2:
-                    put(pi, base + 3 + k, b)
-                    put(am, 3 + k, a)
-                else:
-                    put(pi, base + k, b)
-                    put(pi, base + 6 + k, a)
     for copy in bonds:
         copy.wait()
 
@@ -241,23 +240,23 @@
 
 
 def relax_early(planes, half, first, u, *refs):
-    info, w_in, sx, si, ri, a_old = refs[:6]
+    info, w_in, sx, si, ri, *a_old = refs[: 7 if first else 6]
     a_new, bi = refs[-2:]
     offset = (PIECES if first else 6) * u
     even = parity(info, half)
     weight = weight_of(w_in, None)
     get_b = second_planes(planes, half, sx, si, None, ri, offset, offset)
     if u == 1:
-        bi[pl.ds(0, 6 * half), :] = refs[6][...]
+        bi[pl.ds(0, 6 * half), :] = refs[-3][...]
 
     def get_a(w, k):
         if not first:
-            return tile(a_old, 3 * (w - 1) + k, half)
+            return tile(a_old[0], 3 * (w - 1) + k, half)
         if w == planes - 1:
             return tile(si, offset + 6 + k, half)
         if w == planes:
             return tile(ri, offset + 6 + k, half)
-        return tile(a_old, 3 * (w - 1) + k, half)
+        return tile(a_old[w - 1], k, half)
 
     for w in range(1, planes + 1):
         h = field(get_b, weight, 0, even, w)
@@ -436,6 +435,10 @@
     e_out[...] = mine
 
 
+def total_kernel(sites, parts, total):
+    total[...] = jnp.sum(parts[...], axis=0, keepdims=True) / sites
+
+
 def exchanged(u, info, note):
     place = lax.axis_index("temp")
     upper = slot_of(u) == 1
@@ -449,56 +452,39 @@
     info0, info1, i0, i1, o0, o1, ri0, ri1, ro0, ro1, out_h, taken, out, sems = refs
     core = core_index()
     columns = out.shape[-1]
-    pushes = []
+    sources = []
     for u, info, own, other in ((0, info0, (i0, o0), (ri0, ro0)), (1, info1, (i1, o1), (ri1, ro1))):
-        note = ri0[pl.ds(EARLY * half, 8), :] if u == 0 else ri1[pl.ds(EARLY * half, 8), :]
+        note = other[0][pl.ds(EARLY * half, 8), :]
         take = exchanged(u, info, note)
         taken[u : u + 1, :] = jnp.full((1, columns), take.astype(jnp.int32), jnp.int32)
-
-        def write(early, late, parities):
-            even = (lax.broadcasted_iota(jnp.int32, (half, columns), 1) & 1) == jnp.broadcast_to(
-                parities, (half, columns)
-            )
-            for w in range(planes):
-                z = w + core * (planes - 1 - 2 * w)
-                m = at_plane(even, w)
+        sources.append((take, (*other, note[0:1, :].astype(jnp.int32)), (*own, info[0:1, :])))
+    pushes = []
+    for u, (take, theirs, ours) in enumerate(sources):
+        for w in range(planes):
+            z = w + core * (planes - 1 - 2 * w)
+
+            def write(early, late, parities):
+                lane = lax.broadcasted_iota(jnp.int32, (half, columns), 1)
+                m = at_plane((lane & 1) == jnp.broadcast_to(parities, (half, columns)), w)
                 for k in range(3):
                     a = tile(late, k, half) if w == 0 else tile(early, 3 * (w - 1) + k, half)
                     b = tile(late, 3 + 3 * w + k, half) if w < 2 else tile(early, 3 + 3 * w + k, half)
-                    out[u, k, z, pl.ds(0, half, stride=2), :] = jnp.where(m, a, b)
-                    out[u, k, z, pl.ds(1, half, stride=2), :] = jnp.where(m, b, a)
-
-        @pl.when(take)
-        def _():
-            write(*other, note[0:1, :].astype(jnp.int32))
-
-        @pl.when(jnp.logical_not(take))
-        def _():
-            write(*own, info[0:1, :])
-
-        push = pltpu.make_async_copy(out.at[u], out_h.at[slot_of(u)], sems.at[u])
-        push.start()
-        pushes.append(push)
+                    out[u, w, k, pl.ds(0, half, stride=2), :] = jnp.where(m, a, b)
+                    out[u, w, k, pl.ds(1, half, stride=2), :] = jnp.where(m, b, a)
+
+            pl.when(take)(functools.partial(write, *theirs))
+            pl.when(jnp.logical_not(take))(functools.partial(write, *ours))
+            push = pltpu.make_async_copy(out.at[u, w], out_h.at[slot_of(u), :, z], sems.at[u, w])
+            push.start()
+            pushes.append(push)
     for push in pushes:
         push.wait()
 
 
-def partner_of(u):
-    place, temps = lax.axis_index("temp"), lax.axis_size("temp")
-    odd = lax.rem(place, 2)
-    step = 1 - 2 * odd if u == 0 else 2 * odd - 1
-    return lax.rem(place + step + temps, temps)
-
-
-def energy_kernel(count, sites, taken, parts, energies_h, energies, sem):
-    def total(place):
-        rows = parts[pl.ds(pl.multiple_of(place * count, count), count), :]
-        return jnp.sum(rows, axis=0, keepdims=True) / sites
-
-    own = total(lax.axis_index("temp"))
+def energy_kernel(taken, total, r0, r1, energies_h, energies, sem):
     final = [
-        jnp.where(taken[u : u + 1, u : u + 1] > 0, total(partner_of(u))[:, u : u + 1], own[:, u : u + 1])
-        for u in range(2)
+        jnp.where(taken[u : u + 1, u : u + 1] > 0, r[:, u : u + 1], total[:, u : u + 1])
+        for u, r in ((0, r0), (1, r1))
     ]
     lane = lax.broadcasted_iota(jnp.int32, energies.shape, 1)
     energies[...] = jnp.where(
@@ -538,24 +524,32 @@
 
     spins = PIECES * half
     pair = vm(6 * half, columns)
-    p0x, p1x, pi, am0, am1, info0, info1, beta0, beta1 = kernel_call(
-        functools.partial(load_kernel, planes, half),
-        [vm(spins + 4 * rows, columns), vm(spins, columns), vm(2 * spins + 4 * rows, columns)]
-        + [pair] * 2
+    raw = [in_hbm(v) for v in (swap_bits, colour_order, inverse_temps, spin_state, couplings)]
+    plane = vm(3 * half, columns)
+    scratch = [
+        pltpu.SMEM((replicas,), jnp.int32),
+        pltpu.SMEM((replicas,), jnp.int32),
+        pltpu.SMEM((replicas,), F32),
+        vm(2, replicas, 3, rows, columns),
+        pltpu.SemaphoreType.DMA((5,)),
+        pltpu.SemaphoreType.DMA((4,)),
+    ]
+    p0x, p1x, ax0, ax1, info0, info1, beta0, beta1 = kernel_call(
+        functools.partial(load_kernel, planes, half, False),
+        [vm(spins + 4 * rows, columns), vm(spins, columns), plane, plane]
         + [vm(8, columns, dtype=jnp.int32)] * 2
         + [vm(8, columns)] * 2,
         [HBM] * 5,
-        scratch=[
-            pltpu.SMEM((replicas,), jnp.int32),
-            pltpu.SMEM((replicas,), jnp.int32),
-            pltpu.SMEM((replicas,), F32),
-            vm(planes, replicas, 3, rows, columns),
-            pltpu.SemaphoreType.DMA((3 + planes,)),
-            pltpu.SemaphoreType.DMA((2, 4)),
-        ],
-    )(*(in_hbm(v) for v in (swap_bits, colour_order, inverse_temps, spin_state, couplings)))
+        scratch=scratch,
+    )(*raw)
+    pi, ai0, ai1 = kernel_call(
+        functools.partial(load_kernel, planes, half, True),
+        [vm(2 * spins + 4 * rows, columns), plane, plane],
+        [HBM] * 5,
+        scratch=scratch,
+    )(*raw)
     info, beta = [info0, info1], [beta0, beta1]
-    sx, si, a_in, a_x = [p0x, p1x], [pi, pi], [am0, am1], [[], []]
+    sx, si, a_in, a_x = [p0x, p1x], [pi, pi], [(ax0, ai0), (ax1, ai1)], [[], []]
     rx = [swap_cross(sx[u]) for u in range(2)]
     ri = swap_in(pi)
 
@@ -586,8 +580,8 @@
             new_in[u], bi[u] = kernel_call(
                 functools.partial(relax_early, planes, half, first, u),
                 [vm(3 * planes * half, columns), vm(6 * (1 + u) * half, columns)],
-                [VM] * (6 + u),
-            )(info[u], w_in[u], sx[u], si[u], ri, a_in[u], *bi[:u])
+                [VM] * (6 + first + u),
+            )(info[u], w_in[u], sx[u], si[u], ri, *a_in[u], *bi[:u])
         for u in range(2):
             *a_x[u], sx[u] = kernel_call(
                 functools.partial(relax_late, planes, half, first),
@@ -595,7 +589,7 @@
                 [VM] * (6 if first else 7),
                 scratch=[] if first else [pair],
             )(info[u], w_in[u], w_x[u], sx[u], rx[u], new_in[u], *a_x[u])
-            si[u], a_in[u] = bi[u], new_in[u]
+            si[u], a_in[u] = bi[u], [new_in[u]]
             rx[u] = swap_cross(sx[u])
         ri = swap_in(bi[1])
 
@@ -612,7 +606,7 @@
     for u in range(2):
         outer[u], *energy = kernel_call(
             functools.partial(heat_late, planes, half, u),
-            [vm(LATE * half, columns), vm(temps * count, 2) if u else vm(8, columns)],
+            [vm(LATE * half, columns), vm(count, 2) if u else vm(8, columns)],
             [VM] * (11 + u),
             scratch=[vm(3, half, columns)],
         )(
@@ -621,22 +615,26 @@
         )
         r_outer[u] = away(outer[u], u)
 
-    parts = lax.all_to_all(energy[0], ("temp", "gz"), split_axis=0, concat_axis=0, tiled=True)
+    parts = lax.all_to_all(energy[0], "gz", split_axis=0, concat_axis=0, tiled=True)
+    (total,) = kernel_call(
+        functools.partial(total_kernel, float(columns * rows * planes * count)), [vm(1, 2)], [VM]
+    )(parts)
+    r_total = [away(total, u) for u in range(2)]
 
     spin_final, taken = kernel_call(
         functools.partial(out_kernel, planes, half),
         [jax.ShapeDtypeStruct(spin_state.shape, F32), vm(8, columns, dtype=jnp.int32)],
         [VM] * 10,
         out_specs=[HBM, VM],
-        scratch=[vm(*spin_state.shape), pltpu.SemaphoreType.DMA((2,))],
+        scratch=[vm(2, planes, 3, rows, columns), pltpu.SemaphoreType.DMA((2, planes))],
     )(info0, info1, *inner, *outer, *r_inner, *r_outer)
     (energies,) = kernel_call(
-        functools.partial(energy_kernel, count, float(columns * rows * planes * count)),
+        energy_kernel,
         [jax.ShapeDtypeStruct((1, 2), F32)],
-        [VM] * 2,
+        [VM] * 4,
         out_specs=[HBM],
         scratch=[vm(1, 2), pltpu.SemaphoreType.DMA(())],
-    )(taken, parts)
+    )(taken, total, *r_total)
     return spin_final, energies.reshape(-1)
 
 

time: 91.4 us -> 88.7 us (0.970)
  blocking collectives: 0 us -> 15.6 us
  waiting for transfers between devices: 26.4 us -> 16.7 us
  starting transfers between devices: 49.5 us -> 40.5 us
    all_to_all x0 -> x1, blocking collectives: none -> 15.6 us  [step(): lax.all_to_all(energy[0], 'gz', split_axis=0, concat_axis=0, tiled=True)]
    all_to_all x1 -> x0, waiting for transfers between devices: 12.1 us -> none  [step(): lax.all_to_all(energy[0], ('temp', 'gz'), split_axis=0, concat_axis=0, ti...]
    all_to_all x1 -> x0, starting transfers between devices: 10.3 us -> none  [step(): lax.all_to_all(energy[0], ('temp', 'gz'), split_axis=0, concat_axis=0, ti...]
    ppermute x4 -> x6, starting transfers between devices: 6.14 us -> 8.82 us  [away(): return lax.ppermute(value, 'temp', partners[u])]
    ppermute x7, starting transfers between devices: 32.5 us -> 31.1 us  [swap_cross(): return lax.ppermute(value, 'gz', cross)]
    ppermute x7, waiting for transfers between devices: 14.2 us -> 15.6 us  [swap_cross(): return lax.ppermute(value, 'gz', cross)]
    ppermute x4 -> x6, waiting for transfers between devices: 0.01 us -> 1.1 us  [away(): return lax.ppermute(value, 'temp', partners[u])]
    pallas_call x2 -> x4, Pallas kernels: 2.4 us -> 3.33 us  [the longest x1 1.39 us: step(): kernel_call(functools.partial(load_kernel, planes, half, False), [vm(spin...]
  transfers between devices with their start and end apart: 16 -> 17, of which waited for: 8 -> 8; matrix products, arithmetic and copies ran while one was open for 0% -> 0% of each run, Pallas kernels for 10% -> 12%
where the time goes in v1:
time: 88.7 us; the launch traced here: 88.5 us
  starting transfers between devices  40.5 us (46%)
  waiting for transfers between devices  16.7 us (19%)
  blocking collectives  15.6 us (18%)
  Pallas kernels  14.6 us (16%)
  between operations  1.04 us (1%)
    ppermute x7, starting transfers between devices, swap_cross(): return lax.ppermute(value, 'gz', cross)  31.1 us
    all_to_all x1, blocking collectives, step(): lax.all_to_all(energy[0], 'gz', split_axis=0, concat_axis=0, tiled=True)  15.6 us
    ppermute x7, waiting for transfers between devices, swap_cross(): return lax.ppermute(value, 'gz', cross)  15.6 us
    ppermute x6, starting transfers between devices, away(): return lax.ppermute(value, 'temp', partners[u])  8.82 us
    pallas_call x4, Pallas kernels, step(): kernel_call(functools.partial(relax_early, planes, half, first, u), [vm(3...  2.63 us
    pallas_call x2, Pallas kernels, step(): kernel_call(functools.partial(heat_early, planes, half, u), [vm(EARLY * h...  1.95 us
    pallas_call x4, Pallas kernels, step(): kernel_call(functools.partial(relax_late, planes, half, first), [pair] *...  1.9 us
  transfers between devices with their start and end apart: 17, of which 8 were waited for; matrix products, arithmetic and copies ran while one was open for 0% of the time, Pallas kernels for 12%

profile of v1, /device:TPU:40, one launch (start us, length us, event | category | flops | bytes accessed | tf_op | source)
XLA Modules:
  0.0 88.5 jit_solution(7190857091678756598)
XLA Ops:
  0.6 1.3 %shard_map.96 = (f32[1664,128]{1,0:T(8,128)S(1)}, f32[192,128]{1,0:T(8,128)S(1)}, f32[192,128]{1,0:T(8,128)S(1)}) custom-call(s32[2]{0:T(128)} %swap.1, s32[2]{0:T(128)} %colour.1, f32[2]{0:T(128)} %refs_2_.3, f32[2,3,4,128,128]{4,3,2,1,0:T(8,128)} %refs_3_.3, f32[3,4,128,128]{3,2,1,0:T(8,128)} %refs_0_.7), custom_call_target="tpu_custom_call" | custom-call | tf_op jit(solution)/shard_map/pallas_call | solution.py:545
  2.1 1.4 %shard_map.95 = (f32[1088,128]{1,0:T(8,128)S(1)}, f32[576,128]{1,0:T(8,128)S(1)}, f32[192,128]{1,0:T(8,128)S(1)}, f32[192,128]{1,0:T(8,128)S(1)}, s32[8,128]{1,0...) custom-call(s32[2]{0:T(128)} %swap.1, s32[2]{0:T(128)} %colour.1, f32[2]{0:T(128)} %refs_2_.3, ...), custom_call_target="tpu_custom_call" | custom-call | tf_op jit(solution)/shard_map/pallas_call | solution.py:537
  3.5 22.5 %collective-permute-start.1 = (f32[1088,128]{1,0:T(8,128)S(1)}, f32[1088,128]{1,0:T(8,128)S(1)}, u32[]{:S(2)}, u32[]{:S(2)}) collective-permute-start(f32[1088,128]{1,0:T(8,128)S(1)} %get-tuple-element.50.refs_2_.refs_3_), channel_id=1, source_target_pairs={{0,31},{1,2},{2,1},{3,4},{4,3},{5,6},{6,5},{7,8},{8,7},{9,10},{10,... | collective-permute-start | bytes 1671176 | tf_op jit(solution)/shard_map/ppermute | solution.py:520
  27.8 0.9 %collective-permute-start.4 = (f32[576,128]{1,0:T(8,128)S(1)}, f32[576,128]{1,0:T(8,128)S(1)}, u32[]{:S(2)}, u32[]{:S(2)}) collective-permute-start(f32[576,128]{1,0:T(8,128)S(1)} %get-tuple-element.58.refs_2_.refs_3_), channel_id=1, source_target_pairs={{0,31},{1,2},{2,1},{3,4},{4,3},{5,6},{6,5},{7,8},{8,7},{9,10},{10,... | collective-permute-start | bytes 884744 | tf_op jit(solution)/shard_map/ppermute | solution.py:520
  28.7 4.6 %collective-permute-done.1.refs_1_.refs_4_ = f32[1088,128]{1,0:T(8,128)S(1)} collective-permute-done((f32[1088,128]{1,0:T(8,128)S(1)}, f32[1088,128]{1,0:T(8,128)S(1)}, u32[]{:S(2)}, u32[]{:S(2)}) %collective-permute-start.1) | collective-permute-done | bytes 557088 | tf_op jit(solution)/shard_map/ppermute | solution.py:520
  33.9 2.5 %collective-permute-done.4.refs_4_ = f32[576,128]{1,0:T(8,128)S(1)} collective-permute-done((f32[576,128]{1,0:T(8,128)S(1)}, f32[576,128]{1,0:T(8,128)S(1)}, u32[]{:S(2)}, u32[]{:S(2)}) %collective-permute-start.4) | collective-permute-done | bytes 294944 | tf_op jit(solution)/shard_map/ppermute | solution.py:520
  38.5 3.1 %collective-permute-start.2 = (f32[384,128]{1,0:T(8,128)S(1)}, f32[384,128]{1,0:T(8,128)S(1)}, u32[]{:S(2)}, u32[]{:S(2)}) collective-permute-start(f32[384,128]{1,0:T(8,128)S(1)} %get-tuple-element.55.refs_2_.refs_3_), channel_id=1, source_target_pairs={{0,31},{1,2},{2,1},{3,4},{4,3},{5,6},{6,5},{7,8},{8,7},{9,10},{10,... | collective-permute-start | bytes 589832 | tf_op jit(solution)/shard_map/ppermute | solution.py:520
  41.7 1.4 %shard_map.106 = (f32[4,4,64,128]{3,2,1,0:T(8,128)S(1)}, f32[4,4,64,128]{3,2,1,0:T(8,128)S(1)}, f32[4,4,64,128]{3,2,1,0:T(8,128)S(1)}, f32[4,4,64,128]{3,2,1,0:T...) custom-call(s32[2]{0:T(128)S(1)} %copy-done.4, s32[2]{0:T(128)S(1)} %copy-done.5, ...), custom_call_target="tpu_custom_call" | custom-call | tf_op jit(solution)/shard_map/pallas_call | solution.py:556
  43.3 1.6 %collective-permute-done.2.refs_4_ = f32[384,128]{1,0:T(8,128)S(1)} collective-permute-done((f32[384,128]{1,0:T(8,128)S(1)}, f32[384,128]{1,0:T(8,128)S(1)}, u32[]{:S(2)}, u32[]{:S(2)}) %collective-permute-start.2) | collective-permute-done | bytes 196640 | tf_op jit(solution)/shard_map/ppermute | solution.py:520
  45.4 2.5 %collective-permute-done.7.refs_4_ = f32[384,128]{1,0:T(8,128)S(1)} collective-permute-done((f32[384,128]{1,0:T(8,128)S(1)}, f32[384,128]{1,0:T(8,128)S(1)}, u32[]{:S(2)}, u32[]{:S(2)}) %collective-permute-start.7) | collective-permute-done | bytes 196640 | tf_op jit(solution)/shard_map/ppermute | solution.py:520
  48.4 1.0 %shard_map.107 = (f32[968,128]{1,0:T(8,128)S(1)}, f32[64,128]{1,0:T(8,128)S(1)}) custom-call(s32[8,128]{1,0:T(8,128)S(1)} %get-tuple-element.45.refs_2_.refs_0_, f32[8,128]{1,0:T(8,128)S(1)} %get-tuple-element.47.refs_1_, f32[2,4,6,64,128]{4,3,2,1,0:T(8,128)S(1)} %get-tuple-element.49.refs_1_.refs_2_, f32[384,128]{1,0:T(8,128)S(1)} %shard_map.103.refs_3_.refs_4_, ...), custom_call_target="tpu_custom_call" | custom-call | tf_op jit(solution)/shard_map/pallas_call | solution.py:598
  49.4 1.9 %collective-permute-start.11 = (f32[968,128]{1,0:T(8,128)S(1)}, f32[968,128]{1,0:T(8,128)S(1)}, u32[]{:S(2)}, u32[]{:S(2)}) collective-permute-start(f32[968,128]{1,0:T(8,128)S(1)} %get-tuple-element.72.refs_9_.refs_2_), channel_id=1, source_target_pairs={{0,32},{32,0},{64,96},{96,64},{1,33},{33,1},{65,97},{97,65},{2,34}... | collective-permute-start | bytes 1486856 | tf_op jit(solution)/shard_map/ppermute | solution.py:523
  51.3 1.0 %shard_map.109 = (f32[968,128]{1,0:T(8,128)S(1)}, f32[64,128]{1,0:T(8,128)S(1)}) custom-call(s32[8,128]{1,0:T(8,128)S(1)} %get-tuple-element.46.refs_3_.refs_0_.refs_1_, f32[8,128]{1,0:T(8,128)S(1)} %get-tuple-element.73.refs_1_, f32[2,4,6,64,128]{4,3,2,1,0:T(8,128)S(1)} %get-tuple-element.57.refs_1_.refs_2_, f32[384,128]{1,0:T(8,128)S(1)} %shard_map.108.refs_3_.refs_4_, ...), custom_call_target="tpu_custom_call" | custom-call | tf_op jit(solution)/shard_map/pallas_call | solution.py:598
  52.3 2.4 %collective-permute-start.12 = (f32[968,128]{1,0:T(8,128)S(1)}, f32[968,128]{1,0:T(8,128)S(1)}, u32[]{:S(2)}, u32[]{:S(2)}) collective-permute-start(f32[968,128]{1,0:T(8,128)S(1)} %get-tuple-element.78.refs_9_.refs_3_), channel_id=1, source_target_pairs={{0,96},{32,64},{64,32},{96,0},{1,97},{33,65},{65,33},{97,1},{2,98}... | collective-permute-start | bytes 1486856 | tf_op jit(solution)/shard_map/ppermute | solution.py:523
  54.6 1.5 %collective-permute-start.9 = (f32[384,128]{1,0:T(8,128)S(1)}, f32[384,128]{1,0:T(8,128)S(1)}, u32[]{:S(2)}, u32[]{:S(2)}) collective-permute-start(f32[384,128]{1,0:T(8,128)S(1)} %get-tuple-element.79), channel_id=1, source_target_pairs={{0,31},{1,2},{2,1},{3,4},{4,3},{5,6},{6,5},{7,8},{8,7},{9,10},{10,... | collective-permute-start | bytes 589832 | tf_op jit(solution)/shard_map/ppermute | solution.py:520
  56.2 1.4 %collective-permute-start.8 = (f32[384,128]{1,0:T(8,128)S(1)}, f32[384,128]{1,0:T(8,128)S(1)}, u32[]{:S(2)}, u32[]{:S(2)}) collective-permute-start(f32[384,128]{1,0:T(8,128)S(1)} %shard_map.103.refs_3_.refs_4_), channel_id=1, source_target_pairs={{0,31},{1,2},{2,1},{3,4},{4,3},{5,6},{6,5},{7,8},{8,7},{9,10},{10,... | collective-permute-start | bytes 589832 | tf_op jit(solution)/shard_map/ppermute | solution.py:520
  57.6 1.5 %collective-permute-start.10 = (f32[384,128]{1,0:T(8,128)S(1)}, f32[384,128]{1,0:T(8,128)S(1)}, u32[]{:S(2)}, u32[]{:S(2)}) collective-permute-start(f32[384,128]{1,0:T(8,128)S(1)} %shard_map.108.refs_3_.refs_4_), channel_id=1, source_target_pairs={{0,31},{1,2},{2,1},{3,4},{4,3},{5,6},{6,5},{7,8},{8,7},{9,10},{10,... | collective-permute-start | bytes 589832 | tf_op jit(solution)/shard_map/ppermute | solution.py:520
  59.1 1.8 %collective-permute-done.9.refs_8_ = f32[384,128]{1,0:T(8,128)S(1)} collective-permute-done((f32[384,128]{1,0:T(8,128)S(1)}, f32[384,128]{1,0:T(8,128)S(1)}, u32[]{:S(2)}, u32[]{:S(2)}) %collective-permute-start.9) | collective-permute-done | bytes 196640 | tf_op jit(solution)/shard_map/ppermute | solution.py:520
  60.9 2.1 %collective-permute-done.8.refs_5_ = f32[384,128]{1,0:T(8,128)S(1)} collective-permute-done((f32[384,128]{1,0:T(8,128)S(1)}, f32[384,128]{1,0:T(8,128)S(1)}, u32[]{:S(2)}, u32[]{:S(2)}) %collective-permute-start.8) | collective-permute-done | bytes 196640 | tf_op jit(solution)/shard_map/ppermute | solution.py:520
  65.9 1.1 %collective-permute-start.14 = (f32[576,128]{1,0:T(8,128)S(1)}, f32[576,128]{1,0:T(8,128)S(1)}, u32[]{:S(2)}, u32[]{:S(2)}) collective-permute-start(f32[576,128]{1,0:T(8,128)S(1)} %get-tuple-element.84.refs_5_), channel_id=1, source_target_pairs={{0,96},{32,64},{64,32},{96,0},{1,97},{33,65},{65,33},{97,1},{2,98}... | collective-permute-start | bytes 884744 | tf_op jit(solution)/shard_map/ppermute | solution.py:523
  67.0 15.6 %all_to_all.11 = f32[32,1,2]{2,1,0:T(1,128)S(1)} all-to-all(f32[32,1,2]{2,1,0:T(1,128)S(1)} %bitcast.6), channel_id=1, replica_groups=mesh['group'=2,'temp'=4,'gz'=32] {'gz'}, dimensions={0} | all-to-all | bytes 512 | tf_op jit(solution)/shard_map/all_to_all | solution.py:618
  83.0 2.2 %collective-permute-start.16 = (f32[1,2]{1,0:T(1,128)S(1)}, f32[1,2]{1,0:T(1,128)S(1)}, u32[]{:S(2)}, u32[]{:S(2)}) collective-permute-start(f32[1,2]{1,0:T(1,128)S(1)} %shard_map.113.total), channel_id=1, source_target_pairs={{0,96},{32,64},{64,32},{96,0},{1,97},{33,65},{65,33},{97,1},{2,98}... | collective-permute-start | bytes 32 | tf_op jit(solution)/shard_map/ppermute | solution.py:523
  85.3 1.4 %shard_map.112 = (f32[2,3,4,128,128]{4,3,2,1,0:T(8,128)}, s32[8,128]{1,0:T(8,128)S(1)}) custom-call(s32[8,128]{1,0:T(8,128)S(1)} %get-tuple-element.45.refs_2_.refs_0_, s32[8,128]{1,0:T(8,128)S(1)} %get-tuple-element.46.refs_3_.refs_0_.refs_1_, f32[968,128]{1,0:T(8,128)S(1)} %get-tuple-element.72.refs_9_.refs_2_, ...), custom_call_target="tpu_custom_call" | custom-call | tf_op jit(solution)/shard_map/pallas_call | solution.py:624
  86.7 1.1 %collective-permute-done.16.r1 = f32[1,2]{1,0:T(1,128)S(1)} collective-permute-done((f32[1,2]{1,0:T(1,128)S(1)}, f32[1,2]{1,0:T(1,128)S(1)}, u32[]{:S(2)}, u32[]{:S(2)}) %collective-permute-start.16) | collective-permute-done | bytes 40 | tf_op jit(solution)/shard_map/ppermute | solution.py:523
  (43 shorter events, 9.6 us)
Async XLA Ops:
  2.0 24.1 %copy-start = (f32[3,4,128,128]{3,2,1,0:T(8,128)S(1)}, f32[3,4,128,128]{3,2,1,0:T(8,128)}, u32[]{:S(2)}) copy-start(f32[3,4,128,128]{3,2,1,0:T(8,128)} %refs_0_.7) | copy-start | bytes 2359300
  2.0 24.1 %collective-permute-start = (f32[1664,128]{1,0:T(8,128)S(1)}, f32[1664,128]{1,0:T(8,128)S(1)}, u32[]{:S(2)}, u32[]{:S(2)}) collective-permute-start(f32[1664,128]{1,0:T(8,128)S(1)} %get-tuple-element.48.refs_3_), channel_id=1, source_target_pairs={{0,1},{1,0},{2,3},{3,2},{4,5},{5,4},{6,7},{7,6},{8,9},{9,8},{10,11... | collective-permute-start | bytes 2555912 | tf_op jit(solution)/shard_map/ppermute | solution.py:517
  3.5 29.8 %collective-permute-start.1 = (f32[1088,128]{1,0:T(8,128)S(1)}, f32[1088,128]{1,0:T(8,128)S(1)}, u32[]{:S(2)}, u32[]{:S(2)}) collective-permute-start(f32[1088,128]{1,0:T(8,128)S(1)} %get-tuple-element.50.refs_2_.refs_3_), channel_id=1, source_target_pairs={{0,31},{1,2},{2,1},{3,4},{4,3},{5,6},{6,5},{7,8},{8,7},{9,10},{10,... | collective-permute-start | bytes 1671176 | tf_op jit(solution)/shard_map/ppermute | solution.py:520
  27.7 9.3 %collective-permute-start.3 = (f32[768,128]{1,0:T(8,128)S(1)}, f32[768,128]{1,0:T(8,128)S(1)}, u32[]{:S(2)}, u32[]{:S(2)}) collective-permute-start(f32[768,128]{1,0:T(8,128)S(1)} %get-tuple-element.61.refs_3_), channel_id=1, source_target_pairs={{0,1},{1,0},{2,3},{3,2},{4,5},{5,4},{6,7},{7,6},{8,9},{9,8},{10,11... | collective-permute-start | bytes 1179656 | tf_op jit(solution)/shard_map/ppermute | solution.py:517
  27.8 8.6 %collective-permute-start.4 = (f32[576,128]{1,0:T(8,128)S(1)}, f32[576,128]{1,0:T(8,128)S(1)}, u32[]{:S(2)}, u32[]{:S(2)}) collective-permute-start(f32[576,128]{1,0:T(8,128)S(1)} %get-tuple-element.58.refs_2_.refs_3_), channel_id=1, source_target_pairs={{0,31},{1,2},{2,1},{3,4},{4,3},{5,6},{6,5},{7,8},{8,7},{9,10},{10,... | collective-permute-start | bytes 884744 | tf_op jit(solution)/shard_map/ppermute | solution.py:520
  37.6 4.1 %copy-start.1 = (f32[2,4,128,128]{3,2,1,0:T(8,128)S(1)}, f32[2,4,128,128]{3,2,1,0:T(8,128)}, u32[]{:S(2)}) copy-start(f32[2,4,128,128]{3,2,1,0:T(8,128)} %level.1) | copy-start | bytes 1572868
  37.6 4.1 %copy-start.2 = (f32[2,4,128,128]{3,2,1,0:T(8,128)S(1)}, f32[2,4,128,128]{3,2,1,0:T(8,128)}, u32[]{:S(2)}) copy-start(f32[2,4,128,128]{3,2,1,0:T(8,128)} %height.1) | copy-start | bytes 1572868
  37.7 4.1 %copy-start.3 = (f32[2,4,128,128]{3,2,1,0:T(8,128)S(1)}, f32[2,4,128,128]{3,2,1,0:T(8,128)}, u32[]{:S(2)}) copy-start(f32[2,4,128,128]{3,2,1,0:T(8,128)} %angle.1) | copy-start | bytes 1572868
  37.7 4.1 %copy-start.4 = (s32[2]{0:T(128)S(1)}, s32[2]{0:T(128)}, u32[]{:S(2)}) copy-start(s32[2]{0:T(128)} %swap.1) | copy-start | bytes 28
  37.7 4.1 %copy-start.5 = (s32[2]{0:T(128)S(1)}, s32[2]{0:T(128)}, u32[]{:S(2)}) copy-start(s32[2]{0:T(128)} %colour.1) | copy-start | bytes 28
  38.4 10.0 %collective-permute-start.5 = (f32[768,128]{1,0:T(8,128)S(1)}, f32[768,128]{1,0:T(8,128)S(1)}, u32[]{:S(2)}, u32[]{:S(2)}) collective-permute-start(f32[768,128]{1,0:T(8,128)S(1)} %get-tuple-element.68.refs_4_), channel_id=1, source_target_pairs={{0,1},{1,0},{2,3},{3,2},{4,5},{5,4},{6,7},{7,6},{8,9},{9,8},{10,11... | collective-permute-start | bytes 1179656 | tf_op jit(solution)/shard_map/ppermute | solution.py:517
  38.5 6.4 %collective-permute-start.2 = (f32[384,128]{1,0:T(8,128)S(1)}, f32[384,128]{1,0:T(8,128)S(1)}, u32[]{:S(2)}, u32[]{:S(2)}) collective-permute-start(f32[384,128]{1,0:T(8,128)S(1)} %get-tuple-element.55.refs_2_.refs_3_), channel_id=1, source_target_pairs={{0,31},{1,2},{2,1},{3,4},{4,3},{5,6},{6,5},{7,8},{8,7},{9,10},{10,... | collective-permute-start | bytes 589832 | tf_op jit(solution)/shard_map/ppermute | solution.py:520
  41.6 6.3 %collective-permute-start.7 = (f32[384,128]{1,0:T(8,128)S(1)}, f32[384,128]{1,0:T(8,128)S(1)}, u32[]{:S(2)}, u32[]{:S(2)}) collective-permute-start(f32[384,128]{1,0:T(8,128)S(1)} %get-tuple-element.67.refs_2_.refs_3_), channel_id=1, source_target_pairs={{0,31},{1,2},{2,1},{3,4},{4,3},{5,6},{6,5},{7,8},{8,7},{9,10},{10,... | collective-permute-start | bytes 589832 | tf_op jit(solution)/shard_map/ppermute | solution.py:520
  43.2 5.2 %collective-permute-start.6 = (f32[384,128]{1,0:T(8,128)S(1)}, f32[384,128]{1,0:T(8,128)S(1)}, u32[]{:S(2)}, u32[]{:S(2)}) collective-permute-start(f32[384,128]{1,0:T(8,128)S(1)} %get-tuple-element.71), channel_id=1, source_target_pairs={{0,1},{1,0},{2,3},{3,2},{4,5},{5,4},{6,7},{7,6},{8,9},{9,8},{10,11... | collective-permute-start | bytes 589832 | tf_op jit(solution)/shard_map/ppermute | solution.py:517
  49.4 35.9 %collective-permute-start.11 = (f32[968,128]{1,0:T(8,128)S(1)}, f32[968,128]{1,0:T(8,128)S(1)}, u32[]{:S(2)}, u32[]{:S(2)}) collective-permute-start(f32[968,128]{1,0:T(8,128)S(1)} %get-tuple-element.72.refs_9_.refs_2_), channel_id=1, source_target_pairs={{0,32},{32,0},{64,96},{96,64},{1,33},{33,1},{65,97},{97,65},{2,34}... | collective-permute-start | bytes 1486856 | tf_op jit(solution)/shard_map/ppermute | solution.py:523
  52.3 33.0 %collective-permute-start.12 = (f32[968,128]{1,0:T(8,128)S(1)}, f32[968,128]{1,0:T(8,128)S(1)}, u32[]{:S(2)}, u32[]{:S(2)}) collective-permute-start(f32[968,128]{1,0:T(8,128)S(1)} %get-tuple-element.78.refs_9_.refs_3_), channel_id=1, source_target_pairs={{0,96},{32,64},{64,32},{96,0},{1,97},{33,65},{65,33},{97,1},{2,98}... | collective-permute-start | bytes 1486856 | tf_op jit(solution)/shard_map/ppermute | solution.py:523
  54.6 6.3 %collective-permute-start.9 = (f32[384,128]{1,0:T(8,128)S(1)}, f32[384,128]{1,0:T(8,128)S(1)}, u32[]{:S(2)}, u32[]{:S(2)}) collective-permute-start(f32[384,128]{1,0:T(8,128)S(1)} %get-tuple-element.79), channel_id=1, source_target_pairs={{0,31},{1,2},{2,1},{3,4},{4,3},{5,6},{6,5},{7,8},{8,7},{9,10},{10,... | collective-permute-start | bytes 589832 | tf_op jit(solution)/shard_map/ppermute | solution.py:520
  56.2 6.9 %collective-permute-start.8 = (f32[384,128]{1,0:T(8,128)S(1)}, f32[384,128]{1,0:T(8,128)S(1)}, u32[]{:S(2)}, u32[]{:S(2)}) collective-permute-start(f32[384,128]{1,0:T(8,128)S(1)} %shard_map.103.refs_3_.refs_4_), channel_id=1, source_target_pairs={{0,31},{1,2},{2,1},{3,4},{4,3},{5,6},{6,5},{7,8},{8,7},{9,10},{10,... | collective-permute-start | bytes 589832 | tf_op jit(solution)/shard_map/ppermute | solution.py:520
  57.6 7.6 %collective-permute-start.10 = (f32[384,128]{1,0:T(8,128)S(1)}, f32[384,128]{1,0:T(8,128)S(1)}, u32[]{:S(2)}, u32[]{:S(2)}) collective-permute-start(f32[384,128]{1,0:T(8,128)S(1)} %shard_map.108.refs_3_.refs_4_), channel_id=1, source_target_pairs={{0,31},{1,2},{2,1},{3,4},{4,3},{5,6},{6,5},{7,8},{8,7},{9,10},{10,... | collective-permute-start | bytes 589832 | tf_op jit(solution)/shard_map/ppermute | solution.py:520
  63.8 19.2 %collective-permute-start.13 = (f32[576,128]{1,0:T(8,128)S(1)}, f32[576,128]{1,0:T(8,128)S(1)}, u32[]{:S(2)}, u32[]{:S(2)}) collective-permute-start(f32[576,128]{1,0:T(8,128)S(1)} %get-tuple-element.81.refs_4_), channel_id=1, source_target_pairs={{0,32},{32,0},{64,96},{96,64},{1,33},{33,1},{65,97},{97,65},{2,34}... | collective-permute-start | bytes 884744 | tf_op jit(solution)/shard_map/ppermute | solution.py:523
  65.9 19.3 %collective-permute-start.14 = (f32[576,128]{1,0:T(8,128)S(1)}, f32[576,128]{1,0:T(8,128)S(1)}, u32[]{:S(2)}, u32[]{:S(2)}) collective-permute-start(f32[576,128]{1,0:T(8,128)S(1)} %get-tuple-element.84.refs_5_), channel_id=1, source_target_pairs={{0,96},{32,64},{64,32},{96,0},{1,97},{33,65},{65,33},{97,1},{2,98}... | collective-permute-start | bytes 884744 | tf_op jit(solution)/shard_map/ppermute | solution.py:523
  82.7 4.0 %collective-permute-start.15 = (f32[1,2]{1,0:T(1,128)S(1)}, f32[1,2]{1,0:T(1,128)S(1)}, u32[]{:S(2)}, u32[]{:S(2)}) collective-permute-start(f32[1,2]{1,0:T(1,128)S(1)} %shard_map.113.total), channel_id=1, source_target_pairs={{0,32},{32,0},{64,96},{96,64},{1,33},{33,1},{65,97},{97,65},{2,34}... | collective-permute-start | bytes 32 | tf_op jit(solution)/shard_map/ppermute | solution.py:523
  83.0 4.8 %collective-permute-start.16 = (f32[1,2]{1,0:T(1,128)S(1)}, f32[1,2]{1,0:T(1,128)S(1)}, u32[]{:S(2)}, u32[]{:S(2)}) collective-permute-start(f32[1,2]{1,0:T(1,128)S(1)} %shard_map.113.total), channel_id=1, source_target_pairs={{0,96},{32,64},{64,32},{96,0},{1,97},{33,65},{65,33},{97,1},{2,98}... | collective-permute-start | bytes 32 | tf_op jit(solution)/shard_map/ppermute | solution.py:523

commit v2 on v0

--- a/solution.py
+++ b/solution.py
@@ -436,6 +436,10 @@
     e_out[...] = mine
 
 
+def total_kernel(sites, parts, total):
+    total[...] = jnp.sum(parts[...], axis=0, keepdims=True) / sites
+
+
 def exchanged(u, info, note):
     place = lax.axis_index("temp")
     upper = slot_of(u) == 1
@@ -483,22 +487,10 @@
         push.wait()
 
 
-def partner_of(u):
-    place, temps = lax.axis_index("temp"), lax.axis_size("temp")
-    odd = lax.rem(place, 2)
-    step = 1 - 2 * odd if u == 0 else 2 * odd - 1
-    return lax.rem(place + step + temps, temps)
-
-
-def energy_kernel(count, sites, taken, parts, energies_h, energies, sem):
-    def total(place):
-        rows = parts[pl.ds(pl.multiple_of(place * count, count), count), :]
-        return jnp.sum(rows, axis=0, keepdims=True) / sites
-
-    own = total(lax.axis_index("temp"))
+def energy_kernel(taken, total, r0, r1, energies_h, energies, sem):
     final = [
-        jnp.where(taken[u : u + 1, u : u + 1] > 0, total(partner_of(u))[:, u : u + 1], own[:, u : u + 1])
-        for u in range(2)
+        jnp.where(taken[u : u + 1, u : u + 1] > 0, r[:, u : u + 1], total[:, u : u + 1])
+        for u, r in ((0, r0), (1, r1))
     ]
     lane = lax.broadcasted_iota(jnp.int32, energies.shape, 1)
     energies[...] = jnp.where(
@@ -524,7 +516,7 @@
     cross = [(i, (i + (1 if i % 2 else -1)) % count) for i in range(count)]
     partners = (
         [(i, i ^ 1) for i in range(temps)],
-        [(i, (i + (1 if i % 2 else -1)) % temps) for i in range(temps)],
+        [(i, j) for i in range(temps) if 0 <= (j := i + (1 if i % 2 else -1)) < temps],
     )
 
     def swap_in(value):
@@ -612,7 +604,7 @@
     for u in range(2):
         outer[u], *energy = kernel_call(
             functools.partial(heat_late, planes, half, u),
-            [vm(LATE * half, columns), vm(temps * count, 2) if u else vm(8, columns)],
+            [vm(LATE * half, columns), vm(count, 2) if u else vm(8, columns)],
             [VM] * (11 + u),
             scratch=[vm(3, half, columns)],
         )(
@@ -621,7 +613,11 @@
         )
         r_outer[u] = away(outer[u], u)
 
-    parts = lax.all_to_all(energy[0], ("temp", "gz"), split_axis=0, concat_axis=0, tiled=True)
+    parts = lax.all_to_all(energy[0], "gz", split_axis=0, concat_axis=0, tiled=True)
+    (total,) = kernel_call(
+        functools.partial(total_kernel, float(columns * rows * planes * count)), [vm(1, 2)], [VM]
+    )(parts)
+    r_total = [away(total, u) for u in range(2)]
 
     spin_final, taken = kernel_call(
         functools.partial(out_kernel, planes, half),
@@ -631,12 +627,12 @@
         scratch=[vm(*spin_state.shape), pltpu.SemaphoreType.DMA((2,))],
     )(info0, info1, *inner, *outer, *r_inner, *r_outer)
     (energies,) = kernel_call(
-        functools.partial(energy_kernel, count, float(columns * rows * planes * count)),
+        energy_kernel,
         [jax.ShapeDtypeStruct((1, 2), F32)],
-        [VM] * 2,
+        [VM] * 4,
         out_specs=[HBM],
         scratch=[vm(1, 2), pltpu.SemaphoreType.DMA(())],
-    )(taken, parts)
+    )(taken, total, *r_total)
     return spin_final, energies.reshape(-1)
 
 

time: 91.4 us -> 90.5 us (level)
  the two profiles are of different devices: /device:TPU:40 before, /device:TPU:36 now
where the time goes in v2:
time: 90.5 us; the launch traced here: 90.3 us
  starting transfers between devices  43.3 us (48%)
  waiting for transfers between devices  16.7 us (18%)
  blocking collectives  15.6 us (17%)
  Pallas kernels  13.5 us (15%)
  between operations  1.09 us (1%)
    ppermute x7, starting transfers between devices, swap_cross(): return lax.ppermute(value, 'gz', cross)  32.9 us
    all_to_all x1, blocking collectives, step(): lax.all_to_all(energy[0], 'gz', split_axis=0, concat_axis=0, tiled=True)  15.6 us
    ppermute x7, waiting for transfers between devices, swap_cross(): return lax.ppermute(value, 'gz', cross)  14.6 us
    ppermute x6, starting transfers between devices, away(): return lax.ppermute(value, 'temp', partners[u])  9.77 us
    pallas_call x4, Pallas kernels, step(): kernel_call(functools.partial(relax_early, planes, half, first, u), [vm(3...  2.55 us
    ppermute x6, waiting for transfers between devices, away(): return lax.ppermute(value, 'temp', partners[u])  2.08 us
    pallas_call x2, Pallas kernels, step(): kernel_call(functools.partial(heat_early, planes, half, u), [vm(EARLY * h...  1.94 us
    pallas_call x4, Pallas kernels, step(): kernel_call(functools.partial(relax_late, planes, half, first), [pair] *...  1.85 us
  transfers between devices with their start and end apart: 17, of which 9 were waited for; matrix products, arithmetic and copies ran while one was open for 0% of the time, Pallas kernels for 10%

profile of v2, /device:TPU:36, one launch (start us, length us, event | category | flops | bytes accessed | tf_op | source)
XLA Modules:
  0.0 90.3 jit_solution(6274407340597747709)
XLA Ops:
  0.6 1.8 %shard_map.95 = (f32[1088,128]{1,0:T(8,128)S(1)}, f32[576,128]{1,0:T(8,128)S(1)}, f32[1664,128]{1,0:T(8,128)S(1)}, f32[384,128]{1,0:T(8,128)S(1)}, f32[384,128]{...) custom-call(s32[2]{0:T(128)} %swap.1, s32[2]{0:T(128)} %colour.1, ...), custom_call_target="tpu_custom_call" | custom-call | tf_op jit(solution)/shard_map/pallas_call | solution.py:533
  2.6 22.5 %collective-permute-start.1 = (f32[1088,128]{1,0:T(8,128)S(1)}, f32[1088,128]{1,0:T(8,128)S(1)}, u32[]{:S(2)}, u32[]{:S(2)}) collective-permute-start(f32[1088,128]{1,0:T(8,128)S(1)} %get-tuple-element.48.refs_2_.refs_3_), channel_id=1, source_target_pairs={{0,31},{1,2},{2,1},{3,4},{4,3},{5,6},{6,5},{7,8},{8,7},{9,10},{10,... | collective-permute-start | bytes 1671176 | tf_op jit(solution)/shard_map/ppermute | solution.py:526
  26.7 2.3 %collective-permute-start.4 = (f32[576,128]{1,0:T(8,128)S(1)}, f32[576,128]{1,0:T(8,128)S(1)}, u32[]{:S(2)}, u32[]{:S(2)}) collective-permute-start(f32[576,128]{1,0:T(8,128)S(1)} %get-tuple-element.55.refs_2_.refs_3_), channel_id=1, source_target_pairs={{0,31},{1,2},{2,1},{3,4},{4,3},{5,6},{6,5},{7,8},{8,7},{9,10},{10,... | collective-permute-start | bytes 884744 | tf_op jit(solution)/shard_map/ppermute | solution.py:526
  29.1 3.2 %collective-permute-done.1.refs_1_.refs_4_ = f32[1088,128]{1,0:T(8,128)S(1)} collective-permute-done((f32[1088,128]{1,0:T(8,128)S(1)}, f32[1088,128]{1,0:T(8,128)S(1)}, u32[]{:S(2)}, u32[]{:S(2)}) %collective-permute-start.1) | collective-permute-done | bytes 557088 | tf_op jit(solution)/shard_map/ppermute | solution.py:526
  32.9 2.5 %collective-permute-done.4.refs_4_ = f32[576,128]{1,0:T(8,128)S(1)} collective-permute-done((f32[576,128]{1,0:T(8,128)S(1)}, f32[576,128]{1,0:T(8,128)S(1)}, u32[]{:S(2)}, u32[]{:S(2)}) %collective-permute-start.4) | collective-permute-done | bytes 294944 | tf_op jit(solution)/shard_map/ppermute | solution.py:526
  37.4 3.1 %collective-permute-start.2 = (f32[384,128]{1,0:T(8,128)S(1)}, f32[384,128]{1,0:T(8,128)S(1)}, u32[]{:S(2)}, u32[]{:S(2)}) collective-permute-start(f32[384,128]{1,0:T(8,128)S(1)} %get-tuple-element.52.refs_2_.refs_3_), channel_id=1, source_target_pairs={{0,31},{1,2},{2,1},{3,4},{4,3},{5,6},{6,5},{7,8},{8,7},{9,10},{10,... | collective-permute-start | bytes 589832 | tf_op jit(solution)/shard_map/ppermute | solution.py:526
  40.7 1.4 %shard_map.105 = (f32[4,4,64,128]{3,2,1,0:T(8,128)S(1)}, f32[4,4,64,128]{3,2,1,0:T(8,128)S(1)}, f32[4,4,64,128]{3,2,1,0:T(8,128)S(1)}, f32[4,4,64,128]{3,2,1,0:T...) custom-call(s32[2]{0:T(128)S(1)} %copy-done.4, s32[2]{0:T(128)S(1)} %copy-done.5, ...), custom_call_target="tpu_custom_call" | custom-call | tf_op jit(solution)/shard_map/pallas_call | solution.py:554
  42.3 1.6 %collective-permute-done.2.refs_4_ = f32[384,128]{1,0:T(8,128)S(1)} collective-permute-done((f32[384,128]{1,0:T(8,128)S(1)}, f32[384,128]{1,0:T(8,128)S(1)}, u32[]{:S(2)}, u32[]{:S(2)}) %collective-permute-start.2) | collective-permute-done | bytes 196640 | tf_op jit(solution)/shard_map/ppermute | solution.py:526
  44.4 2.5 %collective-permute-done.7.refs_4_ = f32[384,128]{1,0:T(8,128)S(1)} collective-permute-done((f32[384,128]{1,0:T(8,128)S(1)}, f32[384,128]{1,0:T(8,128)S(1)}, u32[]{:S(2)}, u32[]{:S(2)}) %collective-permute-start.7) | collective-permute-done | bytes 196640 | tf_op jit(solution)/shard_map/ppermute | solution.py:526
  47.3 1.0 %shard_map.106 = (f32[968,128]{1,0:T(8,128)S(1)}, f32[64,128]{1,0:T(8,128)S(1)}) custom-call(s32[8,128]{1,0:T(8,128)S(1)} %get-tuple-element.43.refs_2_.refs_0_, f32[8,128]{1,0:T(8,128)S(1)} %get-tuple-element.45.refs_1_, f32[2,4,6,64,128]{4,3,2,1,0:T(8,128)S(1)} %get-tuple-element.47.refs_1_.refs_2_, f32[384,128]{1,0:T(8,128)S(1)} %shard_map.102.refs_3_.refs_4_, ...), custom_call_target="tpu_custom_call" | custom-call | tf_op jit(solution)/shard_map/pallas_call | solution.py:596
  48.3 1.6 %collective-permute-start.11 = (f32[968,128]{1,0:T(8,128)S(1)}, f32[968,128]{1,0:T(8,128)S(1)}, u32[]{:S(2)}, u32[]{:S(2)}) collective-permute-start(f32[968,128]{1,0:T(8,128)S(1)} %get-tuple-element.68.refs_9_.refs_2_), channel_id=1, source_target_pairs={{0,32},{32,0},{64,96},{96,64},{1,33},{33,1},{65,97},{97,65},{2,34}... | collective-permute-start | bytes 1486856 | tf_op jit(solution)/shard_map/ppermute | solution.py:529
  49.9 1.0 %shard_map.108 = (f32[968,128]{1,0:T(8,128)S(1)}, f32[64,128]{1,0:T(8,128)S(1)}) custom-call(s32[8,128]{1,0:T(8,128)S(1)} %get-tuple-element.44.refs_3_.refs_0_.refs_1_, f32[8,128]{1,0:T(8,128)S(1)} %get-tuple-element.69.refs_1_, f32[2,4,6,64,128]{4,3,2,1,0:T(8,128)S(1)} %get-tuple-element.54.refs_1_.refs_2_, f32[384,128]{1,0:T(8,128)S(1)} %shard_map.107.refs_3_.refs_4_, ...), custom_call_target="tpu_custom_call" | custom-call | tf_op jit(solution)/shard_map/pallas_call | solution.py:596
  50.9 2.0 %collective-permute-start.12 = (f32[968,128]{1,0:T(8,128)S(1)}, f32[968,128]{1,0:T(8,128)S(1)}, u32[]{:S(2)}, u32[]{:S(2)}) collective-permute-start(f32[968,128]{1,0:T(8,128)S(1)} %get-tuple-element.74.refs_9_.refs_3_), channel_id=1, source_target_pairs={{32,64},{64,32},{33,65},{65,33},{34,66},{66,34},{35,67},{67,35},{3... | collective-permute-start | bytes 1486856 | tf_op jit(solution)/shard_map/ppermute | solution.py:529
  52.9 1.9 %collective-permute-start.9 = (f32[384,128]{1,0:T(8,128)S(1)}, f32[384,128]{1,0:T(8,128)S(1)}, u32[]{:S(2)}, u32[]{:S(2)}) collective-permute-start(f32[384,128]{1,0:T(8,128)S(1)} %get-tuple-element.75), channel_id=1, source_target_pairs={{0,31},{1,2},{2,1},{3,4},{4,3},{5,6},{6,5},{7,8},{8,7},{9,10},{10,... | collective-permute-start | bytes 589832 | tf_op jit(solution)/shard_map/ppermute | solution.py:526
  54.8 1.1 %collective-permute-start.8 = (f32[384,128]{1,0:T(8,128)S(1)}, f32[384,128]{1,0:T(8,128)S(1)}, u32[]{:S(2)}, u32[]{:S(2)}) collective-permute-start(f32[384,128]{1,0:T(8,128)S(1)} %shard_map.102.refs_3_.refs_4_), channel_id=1, source_target_pairs={{0,31},{1,2},{2,1},{3,4},{4,3},{5,6},{6,5},{7,8},{8,7},{9,10},{10,... | collective-permute-start | bytes 589832 | tf_op jit(solution)/shard_map/ppermute | solution.py:526
  56.0 1.8 %collective-permute-start.10 = (f32[384,128]{1,0:T(8,128)S(1)}, f32[384,128]{1,0:T(8,128)S(1)}, u32[]{:S(2)}, u32[]{:S(2)}) collective-permute-start(f32[384,128]{1,0:T(8,128)S(1)} %shard_map.107.refs_3_.refs_4_), channel_id=1, source_target_pairs={{0,31},{1,2},{2,1},{3,4},{4,3},{5,6},{6,5},{7,8},{8,7},{9,10},{10,... | collective-permute-start | bytes 589832 | tf_op jit(solution)/shard_map/ppermute | solution.py:526
  57.8 1.5 %collective-permute-done.9.refs_8_ = f32[384,128]{1,0:T(8,128)S(1)} collective-permute-done((f32[384,128]{1,0:T(8,128)S(1)}, f32[384,128]{1,0:T(8,128)S(1)}, u32[]{:S(2)}, u32[]{:S(2)}) %collective-permute-start.9) | collective-permute-done | bytes 196640 | tf_op jit(solution)/shard_map/ppermute | solution.py:526
  59.3 2.1 %collective-permute-done.8.refs_5_ = f32[384,128]{1,0:T(8,128)S(1)} collective-permute-done((f32[384,128]{1,0:T(8,128)S(1)}, f32[384,128]{1,0:T(8,128)S(1)}, u32[]{:S(2)}, u32[]{:S(2)}) %collective-permute-start.8) | collective-permute-done | bytes 196640 | tf_op jit(solution)/shard_map/ppermute | solution.py:526
  62.3 1.2 %collective-permute-done.10.refs_5_ = f32[384,128]{1,0:T(8,128)S(1)} collective-permute-done((f32[384,128]{1,0:T(8,128)S(1)}, f32[384,128]{1,0:T(8,128)S(1)}, u32[]{:S(2)}, u32[]{:S(2)}) %collective-permute-start.10) | collective-permute-done | bytes 196640 | tf_op jit(solution)/shard_map/ppermute | solution.py:526
  64.3 4.0 %collective-permute-start.14 = (f32[576,128]{1,0:T(8,128)S(1)}, f32[576,128]{1,0:T(8,128)S(1)}, u32[]{:S(2)}, u32[]{:S(2)}) collective-permute-start(f32[576,128]{1,0:T(8,128)S(1)} %get-tuple-element.80.refs_5_), channel_id=1, source_target_pairs={{32,64},{64,32},{33,65},{65,33},{34,66},{66,34},{35,67},{67,35},{3... | collective-permute-start | bytes 884744 | tf_op jit(solution)/shard_map/ppermute | solution.py:529
  68.2 15.6 %all_to_all.11 = f32[32,1,2]{2,1,0:T(1,128)S(1)} all-to-all(f32[32,1,2]{2,1,0:T(1,128)S(1)} %bitcast.6), channel_id=1, replica_groups=mesh['group'=2,'temp'=4,'gz'=32] {'gz'}, dimensions={0} | all-to-all | bytes 512 | tf_op jit(solution)/shard_map/all_to_all | solution.py:616
  84.1 2.0 %collective-permute-start.16 = (f32[1,2]{1,0:T(1,128)S(1)}, f32[1,2]{1,0:T(1,128)S(1)}, u32[]{:S(2)}, u32[]{:S(2)}) collective-permute-start(f32[1,2]{1,0:T(1,128)S(1)} %shard_map.112.total), channel_id=1, source_target_pairs={{32,64},{64,32},{33,65},{65,33},{34,66},{66,34},{35,67},{67,35},{3... | collective-permute-start | bytes 32 | tf_op jit(solution)/shard_map/ppermute | solution.py:529
  86.0 1.4 %shard_map.111 = (f32[2,3,4,128,128]{4,3,2,1,0:T(8,128)}, s32[8,128]{1,0:T(8,128)S(1)}) custom-call(s32[8,128]{1,0:T(8,128)S(1)} %get-tuple-element.43.refs_2_.refs_0_, s32[8,128]{1,0:T(8,128)S(1)} %get-tuple-element.44.refs_3_.refs_0_.refs_1_, f32[968,128]{1,0:T(8,128)S(1)} %get-tuple-element.68.refs_9_.refs_2_, ...), custom_call_target="tpu_custom_call" | custom-call | tf_op jit(solution)/shard_map/pallas_call | solution.py:622
  87.6 2.0 %collective-permute-done.16.r1 = f32[1,2]{1,0:T(1,128)S(1)} collective-permute-done((f32[1,2]{1,0:T(1,128)S(1)}, f32[1,2]{1,0:T(1,128)S(1)}, u32[]{:S(2)}, u32[]{:S(2)}) %collective-permute-start.16) | collective-permute-done | bytes 40 | tf_op jit(solution)/shard_map/ppermute | solution.py:529
  (42 shorter events, 8.1 us)
Async XLA Ops:
  0.6 24.4 %copy-start = (f32[3,4,128,128]{3,2,1,0:T(8,128)S(1)}, f32[3,4,128,128]{3,2,1,0:T(8,128)}, u32[]{:S(2)}) copy-start(f32[3,4,128,128]{3,2,1,0:T(8,128)} %refs_0_.5) | copy-start | bytes 2359300
  2.4 22.6 %collective-permute-start = (f32[1664,128]{1,0:T(8,128)S(1)}, f32[1664,128]{1,0:T(8,128)S(1)}, u32[]{:S(2)}, u32[]{:S(2)}) collective-permute-start(f32[1664,128]{1,0:T(8,128)S(1)} %get-tuple-element.46.refs_3_), channel_id=1, source_target_pairs={{0,1},{1,0},{2,3},{3,2},{4,5},{5,4},{6,7},{7,6},{8,9},{9,8},{10,11... | collective-permute-start | bytes 2555912 | tf_op jit(solution)/shard_map/ppermute | solution.py:523
  2.6 29.7 %collective-permute-start.1 = (f32[1088,128]{1,0:T(8,128)S(1)}, f32[1088,128]{1,0:T(8,128)S(1)}, u32[]{:S(2)}, u32[]{:S(2)}) collective-permute-start(f32[1088,128]{1,0:T(8,128)S(1)} %get-tuple-element.48.refs_2_.refs_3_), channel_id=1, source_target_pairs={{0,31},{1,2},{2,1},{3,4},{4,3},{5,6},{6,5},{7,8},{8,7},{9,10},{10,... | collective-permute-start | bytes 1671176 | tf_op jit(solution)/shard_map/ppermute | solution.py:526
  26.6 9.3 %collective-permute-start.3 = (f32[768,128]{1,0:T(8,128)S(1)}, f32[768,128]{1,0:T(8,128)S(1)}, u32[]{:S(2)}, u32[]{:S(2)}) collective-permute-start(f32[768,128]{1,0:T(8,128)S(1)} %get-tuple-element.57.refs_3_), channel_id=1, source_target_pairs={{0,1},{1,0},{2,3},{3,2},{4,5},{5,4},{6,7},{7,6},{8,9},{9,8},{10,11... | collective-permute-start | bytes 1179656 | tf_op jit(solution)/shard_map/ppermute | solution.py:523
  26.7 8.7 %collective-permute-start.4 = (f32[576,128]{1,0:T(8,128)S(1)}, f32[576,128]{1,0:T(8,128)S(1)}, u32[]{:S(2)}, u32[]{:S(2)}) collective-permute-start(f32[576,128]{1,0:T(8,128)S(1)} %get-tuple-element.55.refs_2_.refs_3_), channel_id=1, source_target_pairs={{0,31},{1,2},{2,1},{3,4},{4,3},{5,6},{6,5},{7,8},{8,7},{9,10},{10,... | collective-permute-start | bytes 884744 | tf_op jit(solution)/shard_map/ppermute | solution.py:526
  36.6 4.1 %copy-start.1 = (f32[2,4,128,128]{3,2,1,0:T(8,128)S(1)}, f32[2,4,128,128]{3,2,1,0:T(8,128)}, u32[]{:S(2)}) copy-start(f32[2,4,128,128]{3,2,1,0:T(8,128)} %level.1) | copy-start | bytes 1572868
  36.6 4.1 %copy-start.2 = (f32[2,4,128,128]{3,2,1,0:T(8,128)S(1)}, f32[2,4,128,128]{3,2,1,0:T(8,128)}, u32[]{:S(2)}) copy-start(f32[2,4,128,128]{3,2,1,0:T(8,128)} %height.1) | copy-start | bytes 1572868
  36.6 4.1 %copy-start.3 = (f32[2,4,128,128]{3,2,1,0:T(8,128)S(1)}, f32[2,4,128,128]{3,2,1,0:T(8,128)}, u32[]{:S(2)}) copy-start(f32[2,4,128,128]{3,2,1,0:T(8,128)} %angle.1) | copy-start | bytes 1572868
  36.6 4.1 %copy-start.4 = (s32[2]{0:T(128)S(1)}, s32[2]{0:T(128)}, u32[]{:S(2)}) copy-start(s32[2]{0:T(128)} %swap.1) | copy-start | bytes 28
  36.6 4.1 %copy-start.5 = (s32[2]{0:T(128)S(1)}, s32[2]{0:T(128)}, u32[]{:S(2)}) copy-start(s32[2]{0:T(128)} %colour.1) | copy-start | bytes 28
  37.3 10.0 %collective-permute-start.5 = (f32[768,128]{1,0:T(8,128)S(1)}, f32[768,128]{1,0:T(8,128)S(1)}, u32[]{:S(2)}, u32[]{:S(2)}) collective-permute-start(f32[768,128]{1,0:T(8,128)S(1)} %get-tuple-element.64.refs_4_), channel_id=1, source_target_pairs={{0,1},{1,0},{2,3},{3,2},{4,5},{5,4},{6,7},{7,6},{8,9},{9,8},{10,11... | collective-permute-start | bytes 1179656 | tf_op jit(solution)/shard_map/ppermute | solution.py:523
  37.4 6.4 %collective-permute-start.2 = (f32[384,128]{1,0:T(8,128)S(1)}, f32[384,128]{1,0:T(8,128)S(1)}, u32[]{:S(2)}, u32[]{:S(2)}) collective-permute-start(f32[384,128]{1,0:T(8,128)S(1)} %get-tuple-element.52.refs_2_.refs_3_), channel_id=1, source_target_pairs={{0,31},{1,2},{2,1},{3,4},{4,3},{5,6},{6,5},{7,8},{8,7},{9,10},{10,... | collective-permute-start | bytes 589832 | tf_op jit(solution)/shard_map/ppermute | solution.py:526
  40.5 6.3 %collective-permute-start.7 = (f32[384,128]{1,0:T(8,128)S(1)}, f32[384,128]{1,0:T(8,128)S(1)}, u32[]{:S(2)}, u32[]{:S(2)}) collective-permute-start(f32[384,128]{1,0:T(8,128)S(1)} %get-tuple-element.63.refs_2_.refs_3_), channel_id=1, source_target_pairs={{0,31},{1,2},{2,1},{3,4},{4,3},{5,6},{6,5},{7,8},{8,7},{9,10},{10,... | collective-permute-start | bytes 589832 | tf_op jit(solution)/shard_map/ppermute | solution.py:526
  42.1 5.2 %collective-permute-start.6 = (f32[384,128]{1,0:T(8,128)S(1)}, f32[384,128]{1,0:T(8,128)S(1)}, u32[]{:S(2)}, u32[]{:S(2)}) collective-permute-start(f32[384,128]{1,0:T(8,128)S(1)} %get-tuple-element.67), channel_id=1, source_target_pairs={{0,1},{1,0},{2,3},{3,2},{4,5},{5,4},{6,7},{7,6},{8,9},{9,8},{10,11... | collective-permute-start | bytes 589832 | tf_op jit(solution)/shard_map/ppermute | solution.py:523
  48.3 37.7 %collective-permute-start.11 = (f32[968,128]{1,0:T(8,128)S(1)}, f32[968,128]{1,0:T(8,128)S(1)}, u32[]{:S(2)}, u32[]{:S(2)}) collective-permute-start(f32[968,128]{1,0:T(8,128)S(1)} %get-tuple-element.68.refs_9_.refs_2_), channel_id=1, source_target_pairs={{0,32},{32,0},{64,96},{96,64},{1,33},{33,1},{65,97},{97,65},{2,34}... | collective-permute-start | bytes 1486856 | tf_op jit(solution)/shard_map/ppermute | solution.py:529
  50.9 35.1 %collective-permute-start.12 = (f32[968,128]{1,0:T(8,128)S(1)}, f32[968,128]{1,0:T(8,128)S(1)}, u32[]{:S(2)}, u32[]{:S(2)}) collective-permute-start(f32[968,128]{1,0:T(8,128)S(1)} %get-tuple-element.74.refs_9_.refs_3_), channel_id=1, source_target_pairs={{32,64},{64,32},{33,65},{65,33},{34,66},{66,34},{35,67},{67,35},{3... | collective-permute-start | bytes 1486856 | tf_op jit(solution)/shard_map/ppermute | solution.py:529
  52.9 6.4 %collective-permute-start.9 = (f32[384,128]{1,0:T(8,128)S(1)}, f32[384,128]{1,0:T(8,128)S(1)}, u32[]{:S(2)}, u32[]{:S(2)}) collective-permute-start(f32[384,128]{1,0:T(8,128)S(1)} %get-tuple-element.75), channel_id=1, source_target_pairs={{0,31},{1,2},{2,1},{3,4},{4,3},{5,6},{6,5},{7,8},{8,7},{9,10},{10,... | collective-permute-start | bytes 589832 | tf_op jit(solution)/shard_map/ppermute | solution.py:526
  54.8 6.6 %collective-permute-start.8 = (f32[384,128]{1,0:T(8,128)S(1)}, f32[384,128]{1,0:T(8,128)S(1)}, u32[]{:S(2)}, u32[]{:S(2)}) collective-permute-start(f32[384,128]{1,0:T(8,128)S(1)} %shard_map.102.refs_3_.refs_4_), channel_id=1, source_target_pairs={{0,31},{1,2},{2,1},{3,4},{4,3},{5,6},{6,5},{7,8},{8,7},{9,10},{10,... | collective-permute-start | bytes 589832 | tf_op jit(solution)/shard_map/ppermute | solution.py:526
  56.0 7.6 %collective-permute-start.10 = (f32[384,128]{1,0:T(8,128)S(1)}, f32[384,128]{1,0:T(8,128)S(1)}, u32[]{:S(2)}, u32[]{:S(2)}) collective-permute-start(f32[384,128]{1,0:T(8,128)S(1)} %shard_map.107.refs_3_.refs_4_), channel_id=1, source_target_pairs={{0,31},{1,2},{2,1},{3,4},{4,3},{5,6},{6,5},{7,8},{8,7},{9,10},{10,... | collective-permute-start | bytes 589832 | tf_op jit(solution)/shard_map/ppermute | solution.py:526
  62.2 21.9 %collective-permute-start.13 = (f32[576,128]{1,0:T(8,128)S(1)}, f32[576,128]{1,0:T(8,128)S(1)}, u32[]{:S(2)}, u32[]{:S(2)}) collective-permute-start(f32[576,128]{1,0:T(8,128)S(1)} %get-tuple-element.77.refs_4_), channel_id=1, source_target_pairs={{0,32},{32,0},{64,96},{96,64},{1,33},{33,1},{65,97},{97,65},{2,34}... | collective-permute-start | bytes 884744 | tf_op jit(solution)/shard_map/ppermute | solution.py:529
  64.3 21.7 %collective-permute-start.14 = (f32[576,128]{1,0:T(8,128)S(1)}, f32[576,128]{1,0:T(8,128)S(1)}, u32[]{:S(2)}, u32[]{:S(2)}) collective-permute-start(f32[576,128]{1,0:T(8,128)S(1)} %get-tuple-element.80.refs_5_), channel_id=1, source_target_pairs={{32,64},{64,32},{33,65},{65,33},{34,66},{66,34},{35,67},{67,35},{3... | collective-permute-start | bytes 884744 | tf_op jit(solution)/shard_map/ppermute | solution.py:529
  83.9 3.7 %collective-permute-start.15 = (f32[1,2]{1,0:T(1,128)S(1)}, f32[1,2]{1,0:T(1,128)S(1)}, u32[]{:S(2)}, u32[]{:S(2)}) collective-permute-start(f32[1,2]{1,0:T(1,128)S(1)} %shard_map.112.total), channel_id=1, source_target_pairs={{0,32},{32,0},{64,96},{96,64},{1,33},{33,1},{65,97},{97,65},{2,34}... | collective-permute-start | bytes 32 | tf_op jit(solution)/shard_map/ppermute | solution.py:529
  84.1 5.5 %collective-permute-start.16 = (f32[1,2]{1,0:T(1,128)S(1)}, f32[1,2]{1,0:T(1,128)S(1)}, u32[]{:S(2)}, u32[]{:S(2)}) collective-permute-start(f32[1,2]{1,0:T(1,128)S(1)} %shard_map.112.total), channel_id=1, source_target_pairs={{32,64},{64,32},{33,65},{65,33},{34,66},{66,34},{35,67},{67,35},{3... | collective-permute-start | bytes 32 | tf_op jit(solution)/shard_map/ppermute | solution.py:529
